TPU v7x, 8 devices: a whole 2x2x1 slice. The times are simulated.
8 devices in a mesh: pp: 2 (over z, y), dp: 4 (over x, core).
Axes of the slice: x: 2, y: 2, z: 1, core: 2. Of those that a mesh axis runs over, the one named last changes fastest.
Arguments:
- act_in: bfloat16 [4, 24, 256, 768], P(None, 'dp')
- loss_seed: bfloat16 [4, 24, 256, 768], P(None, 'dp')
- w_qkv: bfloat16 [2, 768, 36, 64], P('pp', 'dp')
- w_proj: bfloat16 [2, 768, 768], P('pp', 'dp')
- w_up: bfloat16 [2, 768, 3072], P('pp', 'dp')
- w_down: bfloat16 [2, 3072, 768], P('pp', 'dp')
Outputs:
- output 1: float32 [2, 768, 36, 64], P('pp', 'dp')
- output 2: float32 [2, 768, 768], P('pp', 'dp')
- output 3: float32 [2, 768, 3072], P('pp', 'dp')
- output 4: float32 [2, 3072, 768], P('pp', 'dp')
- output 5: bfloat16 [4, 24, 256, 768], P(None, 'dp', 'pp')
All inputs are finite; a program needn't handle non-finite values.
Results may differ from a plain program's by a relative error of at most 0.02.
Values are sent between devices in bfloat16 or wider.
A program may use at most 1 GiB of HBM per device.

v0:
```python
import jax
import jax.numpy as jnp
from jax import lax
from jax.sharding import PartitionSpec as P

NORM_EPS = 1e-6


def rms_norm(hidden):
    return hidden * lax.rsqrt(jnp.mean(hidden * hidden, axis=-1, keepdims=True) + NORM_EPS)


def gelu_tanh(pre_act):
    return jax.nn.gelu(pre_act, approximate=True)


def attn_core(q_heads, k_heads, v_heads):
    seq_len = q_heads.shape[1]
    scores = jnp.einsum('bqnh,bknh->bnqk', q_heads, k_heads, preferred_element_type=jnp.float32) * (q_heads.shape[-1] ** -0.5)
    causal = jnp.arange(seq_len)[:, None] >= jnp.arange(seq_len)[None, :]
    prob_bf = jax.nn.softmax(jnp.where(causal, scores, -1e30), axis=-1).astype(jnp.bfloat16)
    return jnp.einsum('bnqk,bknh->bqnh', prob_bf, v_heads, preferred_element_type=jnp.float32).astype(jnp.bfloat16)


def layer_forward(hidden, w_qkv, w_proj, w_up, w_down):
    num_heads = w_qkv.shape[1] // 3
    hid_f32 = hidden.astype(jnp.float32)
    normed = rms_norm(hid_f32).astype(jnp.bfloat16)
    qkv_act = jnp.einsum('bsd,dnh->bsnh', normed, w_qkv, preferred_element_type=jnp.float32).astype(jnp.bfloat16)
    q_heads = qkv_act[:, :, :num_heads]
    k_heads = qkv_act[:, :, num_heads:2 * num_heads]
    v_heads = qkv_act[:, :, 2 * num_heads:]
    attn_flat = attn_core(q_heads, k_heads, v_heads).reshape(hidden.shape)
    mid_f32 = (hid_f32 + jnp.einsum('bse,ed->bsd', attn_flat, w_proj, preferred_element_type=jnp.float32)).astype(jnp.bfloat16).astype(jnp.float32)
    normed2 = rms_norm(mid_f32).astype(jnp.bfloat16)
    up_act = jnp.einsum('bsd,df->bsf', normed2, w_up, preferred_element_type=jnp.float32).astype(jnp.bfloat16)
    gelu_out = gelu_tanh(up_act.astype(jnp.float32)).astype(jnp.bfloat16)
    block_out = (mid_f32 + jnp.einsum('bsf,fd->bsd', gelu_out, w_down, preferred_element_type=jnp.float32)).astype(jnp.bfloat16)
    saved_acts = (hid_f32, normed, q_heads, k_heads, v_heads, attn_flat, mid_f32, normed2, up_act, gelu_out)
    return block_out, saved_acts


def layer_backward(saved_acts, ct_out, w_qkv, w_proj, w_up, w_down):
    hid_f32, normed, q_heads, k_heads, v_heads, attn_flat, mid_f32, normed2, up_act, gelu_out = saved_acts
    g_down = jnp.einsum('bsf,bsd->fd', gelu_out, ct_out, preferred_element_type=jnp.float32)
    ct_gelu = jnp.einsum('bsd,fd->bsf', ct_out, w_down, preferred_element_type=jnp.float32).astype(jnp.bfloat16)
    gelu_pull = jax.vjp(gelu_tanh, up_act.astype(jnp.float32))[1]
    ct_up = gelu_pull(ct_gelu.astype(jnp.float32))[0].astype(jnp.bfloat16)
    g_up = jnp.einsum('bsd,bsf->df', normed2, ct_up, preferred_element_type=jnp.float32)
    ct_norm2 = jnp.einsum('bsf,df->bsd', ct_up, w_up, preferred_element_type=jnp.float32).astype(jnp.bfloat16)
    norm_pull2 = jax.vjp(rms_norm, mid_f32)[1]
    ct_mid = (ct_out.astype(jnp.float32) + norm_pull2(ct_norm2.astype(jnp.float32))[0]).astype(jnp.bfloat16)
    g_proj = jnp.einsum('bse,bsd->ed', attn_flat, ct_mid, preferred_element_type=jnp.float32)
    ct_attn = jnp.einsum('bsd,ed->bse', ct_mid, w_proj, preferred_element_type=jnp.float32).astype(jnp.bfloat16)
    attn_pull = jax.vjp(attn_core, q_heads, k_heads, v_heads)[1]
    ct_q, ct_k, ct_v = attn_pull(ct_attn.reshape(q_heads.shape))
    ct_qkv = jnp.concatenate([ct_q, ct_k, ct_v], axis=2)
    g_qkv = jnp.einsum('bsd,bsnh->dnh', normed, ct_qkv, preferred_element_type=jnp.float32)
    ct_norm = jnp.einsum('bsnh,dnh->bsd', ct_qkv, w_qkv, preferred_element_type=jnp.float32).astype(jnp.bfloat16)
    norm_pull = jax.vjp(rms_norm, hid_f32)[1]
    ct_hidden = (ct_mid.astype(jnp.float32) + norm_pull(ct_norm.astype(jnp.float32))[0]).astype(jnp.bfloat16)
    return ct_hidden, (g_qkv, g_proj, g_up, g_down)


def stage_forward(hidden, weights):
    for layer_idx in range(weights[0].shape[0]):
        hidden = layer_forward(hidden, weights[0][layer_idx], weights[1][layer_idx], weights[2][layer_idx], weights[3][layer_idx])[0]
    return hidden


def stage_backward(hidden, ct_out, weights):
    num_layers = weights[0].shape[0]
    saved_list = []
    for layer_idx in range(num_layers):
        layer_w = tuple(w_full[layer_idx] for w_full in weights)
        hidden, saved_acts = layer_forward(hidden, *layer_w)
        saved_list.append(saved_acts)
    grad_lists = ([], [], [], [])
    for layer_idx in reversed(range(num_layers)):
        layer_w = tuple(w_full[layer_idx] for w_full in weights)
        ct_out, layer_grads = layer_backward(saved_list[layer_idx], ct_out, *layer_w)
        for grad_list, grad_part in zip(grad_lists, layer_grads):
            grad_list.append(grad_part)
    return ct_out, tuple(jnp.stack(grad_list[::-1]) for grad_list in grad_lists)


def solution(mesh):
    stages = mesh.shape['pp']
    fwd_pairs = [(src_idx, src_idx + 1) for src_idx in range(stages - 1)]
    bwd_pairs = [(src_idx + 1, src_idx) for src_idx in range(stages - 1)]

    def device_step(act_in, loss_seed, w_qkv, w_proj, w_up, w_down):
        num_micro = act_in.shape[0]
        num_ticks = num_micro + 2 * stages - 2
        stage_idx = lax.axis_index('pp')
        weights = tuple(lax.all_gather(w_part, 'dp', axis=1, tiled=True) for w_part in (w_qkv, w_proj, w_up, w_down))
        zero_act = jnp.zeros(act_in.shape[1:], jnp.bfloat16)
        grad_init = tuple(jnp.zeros(w_full.shape, jnp.float32) for w_full in weights)

        def run_forward(hidden):
            return stage_forward(hidden, weights)

        def run_backward(hidden, ct_out, grad_acc):
            ct_in, stage_grads = stage_backward(hidden, ct_out, weights)
            return ct_in, tuple(acc_part + grad_part for acc_part, grad_part in zip(grad_acc, stage_grads))

        def skip_backward(hidden, ct_out, grad_acc):
            return jnp.zeros_like(hidden), grad_acc

        def run_tick(tick_idx, loop_state):
            fwd_buf, bwd_buf, stash_in, outputs, grad_acc = loop_state
            fwd_idx = tick_idx - stage_idx
            fwd_ok = (fwd_idx >= 0) & (fwd_idx < num_micro)
            fwd_slot = jnp.clip(fwd_idx, 0, num_micro - 1)
            fresh_in = lax.dynamic_index_in_dim(act_in, fwd_slot, 0, keepdims=False)
            stage_in = jnp.where(stage_idx == 0, fresh_in, fwd_buf)
            stage_out = lax.cond(fwd_ok, run_forward, jnp.zeros_like, stage_in)
            old_in = lax.dynamic_index_in_dim(stash_in, fwd_slot, 0, keepdims=False)
            stash_in = lax.dynamic_update_index_in_dim(stash_in, jnp.where(fwd_ok, stage_in, old_in), fwd_slot, 0)
            old_out = lax.dynamic_index_in_dim(outputs, fwd_slot, 0, keepdims=False)
            outputs = lax.dynamic_update_index_in_dim(outputs, jnp.where(fwd_ok, stage_out, old_out), fwd_slot, 0)
            bwd_idx = tick_idx - (2 * stages - 2) + stage_idx
            bwd_ok = (bwd_idx >= 0) & (bwd_idx < num_micro)
            bwd_slot = jnp.clip(bwd_idx, 0, num_micro - 1)
            seed_now = lax.dynamic_index_in_dim(loss_seed, bwd_slot, 0, keepdims=False)
            ct_out = jnp.where(stage_idx == stages - 1, seed_now, bwd_buf)
            saved_in = lax.dynamic_index_in_dim(stash_in, bwd_slot, 0, keepdims=False)
            ct_in, grad_acc = lax.cond(bwd_ok, run_backward, skip_backward, saved_in, ct_out, grad_acc)
            fwd_buf = lax.ppermute(stage_out, 'pp', fwd_pairs)
            bwd_buf = lax.ppermute(ct_in, 'pp', bwd_pairs)
            return fwd_buf, bwd_buf, stash_in, outputs, grad_acc

        loop_init = (zero_act, zero_act, jnp.zeros_like(act_in), jnp.zeros_like(act_in), grad_init)
        loop_state = lax.fori_loop(0, num_ticks, run_tick, loop_init)
        outputs, grad_acc = loop_state[3], loop_state[4]
        grad_shards = tuple(lax.psum_scatter(acc_part, 'dp', scatter_dimension=1, tiled=True) for acc_part in grad_acc)
        last_out = jnp.where(stage_idx == stages - 1, outputs, jnp.zeros_like(outputs))
        out_shard = lax.psum_scatter(last_out, 'pp', scatter_dimension=2, tiled=True)
        return grad_shards + (out_shard,)

    weight_spec = P('pp', 'dp')
    act_spec = P(None, 'dp')
    return jax.shard_map(device_step, mesh=mesh, in_specs=(act_spec, act_spec, weight_spec, weight_spec, weight_spec, weight_spec), out_specs=(weight_spec, weight_spec, weight_spec, weight_spec, P(None, 'dp', 'pp')), check_vma=False)
```

profile of v0, /device:TPU:0, one launch (start us, length us, event | category | flops | bytes accessed | tf_op | source)
XLA Modules:
  0.0 2448.5 jit_solution(5655850242696137357)
XLA Ops:
  13.4 53.6 %all-gather.5.cloned.1.call-done = bf16[1,768,36,64]{3,2,0,1:T(8,128)(2,1)} async-done(((bf16[1,192,36,64]{3,2,0,1:T(8,128)(2,1)}), bf16[1,768,36,64]{3,2,0,1:T(8,128)(2,1)}) %all-gather.5.cloned.1.call-update) | async-done | bytes 3538960 | tf_op jit(solution)/shard_map/all_gather | solution.py:96
  83.0 36.1 %all-gather.11.cloned.1.call-done = bf16[1,3072,768]{2,1,0:T(8,128)(2,1)} async-done(((bf16[1,768,768]{2,1,0:T(8,128)(2,1)}), bf16[1,3072,768]{2,1,0:T(8,128)(2,1)}) %all-gather.11.cloned.1.call-update) | async-done | bytes 4718608 | tf_op jit(solution)/shard_map/all_gather | solution.py:96
  119.1 35.9 %all-gather.9.cloned.1.call-done = bf16[1,768,3072]{2,1,0:T(8,128)(2,1)} async-done(((bf16[1,192,3072]{2,1,0:T(8,128)(2,1)}), bf16[1,768,3072]{2,1,0:T(8,128)(2,1)}) %all-gather.9.cloned.1.call-update) | async-done | bytes 4718608 | tf_op jit(solution)/shard_map/all_gather | solution.py:96
  181.5 1885.0 %while.29 = (s32[]{:T(128)}, bf16[6,256,768]{2,1,0:T(8,128)(2,1)}, bf16[6,256,768]{2,1,0:T(8,128)(2,1)}, bf16[4,6,256,768]{3,2,1,0:T(8,128)(2,1)}, bf16[4,6,256,...) while((s32[]{:T(128)}, bf16[6,256,768]{2,1,0:T(8,128)(2,1)}, ...), condition=%wide.region_16.17_spmd, body=%wide.region_0.16_spmd.sunk | while | flops 85058715648 | bytes 869930688 | solution.py:134
  198.0 79.1 %conditional.4 = (bf16[6,256,768]{2,1,0:T(8,128)(2,1)S(1)}) conditional(s32[]{:T(128)} %convert_element_type.472, () %tuple.77, (bf16[6,256,768]{2,1,0:T(8,128)(2,1)}, bf16[1,768,36,64]{1,3,2,0:T(8,128)(2,1)}, bf16[1,768,768]{2,1,0:T(8,128)(2,1)}, bf16[1,768,3072]{2,1,0:T(8,128)(2,1)}, bf16[1,3072,768]{2,1,0:T(8,128)(2,1)}) %tuple.78), branch_computations={%region_1.1_spmd, %region_2.6_spmd} | conditional | flops 23066906624 | bytes 174915680 | solution.py:117
  283.6 46.0 %collective-permute-done = bf16[6,256,768]{2,1,0:T(8,128)(2,1)} collective-permute-done((bf16[6,256,768]{2,1,0:T(8,128)(2,1)S(1)}, bf16[6,256,768]{2,1,0:T(8,128)(2,1)}, u32[]{:S(2)}, u32[]{:S(2)}) %collective-permute-start) | collective-permute-done | bytes 2359328 | tf_op jit(solution)/shard_map/while/body/eval_jaxpr/ppermute | solution.py:129
  346.1 79.1 %conditional.4 = (bf16[6,256,768]{2,1,0:T(8,128)(2,1)S(1)}) conditional(s32[]{:T(128)} %convert_element_type.472, () %tuple.77, (bf16[6,256,768]{2,1,0:T(8,128)(2,1)}, bf16[1,768,36,64]{1,3,2,0:T(8,128)(2,1)}, bf16[1,768,768]{2,1,0:T(8,128)(2,1)}, bf16[1,768,3072]{2,1,0:T(8,128)(2,1)}, bf16[1,3072,768]{2,1,0:T(8,128)(2,1)}) %tuple.78), branch_computations={%region_1.1_spmd, %region_2.6_spmd} | conditional | flops 23066906624 | bytes 174915680 | solution.py:117
  425.3 218.4 %collective-permute-start = (bf16[6,256,768]{2,1,0:T(8,128)(2,1)S(1)}, bf16[6,256,768]{2,1,0:T(8,128)(2,1)}, u32[]{:S(2)}, u32[]{:S(2)}) collective-permute-start(bf16[6,256,768]{2,1,0:T(8,128)(2,1)S(1)} %get-tuple-element.842), channel_id=1, source_target_pairs={{0,4},{1,5},{2,6},{3,7}} | collective-permute-start | bytes 7077896 | tf_op jit(solution)/shard_map/while/body/eval_jaxpr/ppermute | solution.py:129
  647.4 45.2 %collective-permute-done = bf16[6,256,768]{2,1,0:T(8,128)(2,1)} collective-permute-done((bf16[6,256,768]{2,1,0:T(8,128)(2,1)S(1)}, bf16[6,256,768]{2,1,0:T(8,128)(2,1)}, u32[]{:S(2)}, u32[]{:S(2)}) %collective-permute-start) | collective-permute-done | bytes 2359328 | tf_op jit(solution)/shard_map/while/body/eval_jaxpr/ppermute | solution.py:129
  699.6 219.8 %conditional.5 = (bf16[6,256,768]{2,1,0:T(8,128)(2,1)}, f32[1,768,36,64]{1,3,2,0:T(8,128)}, f32[1,768,768]{2,1,0:T(8,128)}, f32[1,768,3072]{2,1,0:T(8,128)}, f32[1,3072,768]{2,1,0:T(8,128)}) conditional(s32[]{:T(128)} %convert_element_type.473, (f32[1,768,36,64]{1,3,2,0:T(8,128)}, f32[1,768,768]{2,1,0:T(8,128)}, f32[1,768,3072]{2,1,0:T(8,128)}, ...), branch_computations={%region_7.7_spmd, %region_8.15_spmd} | conditional | flops 61988265984 | bytes 647828032 | solution.py:128
  920.7 78.9 %conditional.4 = (bf16[6,256,768]{2,1,0:T(8,128)(2,1)S(1)}) conditional(s32[]{:T(128)} %convert_element_type.472, () %tuple.77, (bf16[6,256,768]{2,1,0:T(8,128)(2,1)}, bf16[1,768,36,64]{1,3,2,0:T(8,128)(2,1)}, bf16[1,768,768]{2,1,0:T(8,128)(2,1)}, bf16[1,768,3072]{2,1,0:T(8,128)(2,1)}, bf16[1,3072,768]{2,1,0:T(8,128)(2,1)}) %tuple.78), branch_computations={%region_1.1_spmd, %region_2.6_spmd} | conditional | flops 23066906624 | bytes 174915680 | solution.py:117
  1010.9 44.4 %collective-permute-done = bf16[6,256,768]{2,1,0:T(8,128)(2,1)} collective-permute-done((bf16[6,256,768]{2,1,0:T(8,128)(2,1)S(1)}, bf16[6,256,768]{2,1,0:T(8,128)(2,1)}, u32[]{:S(2)}, u32[]{:S(2)}) %collective-permute-start) | collective-permute-done | bytes 2359328 | tf_op jit(solution)/shard_map/while/body/eval_jaxpr/ppermute | solution.py:129
  1062.6 219.2 %conditional.5 = (bf16[6,256,768]{2,1,0:T(8,128)(2,1)}, f32[1,768,36,64]{1,3,2,0:T(8,128)}, f32[1,768,768]{2,1,0:T(8,128)}, f32[1,768,3072]{2,1,0:T(8,128)}, f32[1,3072,768]{2,1,0:T(8,128)}) conditional(s32[]{:T(128)} %convert_element_type.473, (f32[1,768,36,64]{1,3,2,0:T(8,128)}, f32[1,768,768]{2,1,0:T(8,128)}, f32[1,768,3072]{2,1,0:T(8,128)}, ...), branch_computations={%region_7.7_spmd, %region_8.15_spmd} | conditional | flops 61988265984 | bytes 647828032 | solution.py:128
  1283.2 79.0 %conditional.4 = (bf16[6,256,768]{2,1,0:T(8,128)(2,1)S(1)}) conditional(s32[]{:T(128)} %convert_element_type.472, () %tuple.77, (bf16[6,256,768]{2,1,0:T(8,128)(2,1)}, bf16[1,768,36,64]{1,3,2,0:T(8,128)(2,1)}, bf16[1,768,768]{2,1,0:T(8,128)(2,1)}, bf16[1,768,3072]{2,1,0:T(8,128)(2,1)}, bf16[1,3072,768]{2,1,0:T(8,128)(2,1)}) %tuple.78), branch_computations={%region_1.1_spmd, %region_2.6_spmd} | conditional | flops 23066906624 | bytes 174915680 | solution.py:117
  1373.3 43.6 %collective-permute-done = bf16[6,256,768]{2,1,0:T(8,128)(2,1)} collective-permute-done((bf16[6,256,768]{2,1,0:T(8,128)(2,1)S(1)}, bf16[6,256,768]{2,1,0:T(8,128)(2,1)}, u32[]{:S(2)}, u32[]{:S(2)}) %collective-permute-start) | collective-permute-done | bytes 2359328 | tf_op jit(solution)/shard_map/while/body/eval_jaxpr/ppermute | solution.py:129
  1424.0 219.9 %conditional.5 = (bf16[6,256,768]{2,1,0:T(8,128)(2,1)}, f32[1,768,36,64]{1,3,2,0:T(8,128)}, f32[1,768,768]{2,1,0:T(8,128)}, f32[1,768,3072]{2,1,0:T(8,128)}, f32[1,3072,768]{2,1,0:T(8,128)}) conditional(s32[]{:T(128)} %convert_element_type.473, (f32[1,768,36,64]{1,3,2,0:T(8,128)}, f32[1,768,768]{2,1,0:T(8,128)}, f32[1,768,3072]{2,1,0:T(8,128)}, ...), branch_computations={%region_7.7_spmd, %region_8.15_spmd} | conditional | flops 61988265984 | bytes 647828032 | solution.py:128
  1653.8 77.7 %collective-permute-start = (bf16[6,256,768]{2,1,0:T(8,128)(2,1)S(1)}, bf16[6,256,768]{2,1,0:T(8,128)(2,1)}, u32[]{:S(2)}, u32[]{:S(2)}) collective-permute-start(bf16[6,256,768]{2,1,0:T(8,128)(2,1)S(1)} %get-tuple-element.842), channel_id=1, source_target_pairs={{0,4},{1,5},{2,6},{3,7}} | collective-permute-start | bytes 7077896 | tf_op jit(solution)/shard_map/while/body/eval_jaxpr/ppermute | solution.py:129
  1735.2 42.7 %collective-permute-done = bf16[6,256,768]{2,1,0:T(8,128)(2,1)} collective-permute-done((bf16[6,256,768]{2,1,0:T(8,128)(2,1)S(1)}, bf16[6,256,768]{2,1,0:T(8,128)(2,1)}, u32[]{:S(2)}, u32[]{:S(2)}) %collective-permute-start) | collective-permute-done | bytes 2359328 | tf_op jit(solution)/shard_map/while/body/eval_jaxpr/ppermute | solution.py:129
  1785.2 219.2 %conditional.5 = (bf16[6,256,768]{2,1,0:T(8,128)(2,1)}, f32[1,768,36,64]{1,3,2,0:T(8,128)}, f32[1,768,768]{2,1,0:T(8,128)}, f32[1,768,3072]{2,1,0:T(8,128)}, f32[1,3072,768]{2,1,0:T(8,128)}) conditional(s32[]{:T(128)} %convert_element_type.473, (f32[1,768,36,64]{1,3,2,0:T(8,128)}, f32[1,768,768]{2,1,0:T(8,128)}, f32[1,768,3072]{2,1,0:T(8,128)}, ...), branch_computations={%region_7.7_spmd, %region_8.15_spmd} | conditional | flops 61988265984 | bytes 647828032 | solution.py:128
  2021.1 34.8 %collective-permute-done.1 = bf16[6,256,768]{2,1,0:T(8,128)(2,1)} collective-permute-done((bf16[6,256,768]{2,1,0:T(8,128)(2,1)}, bf16[6,256,768]{2,1,0:T(8,128)(2,1)}, u32[]{:S(2)}, u32[]{:S(2)}) %collective-permute-start.1) | collective-permute-done | bytes 2359328 | tf_op jit(solution)/shard_map/while/body/eval_jaxpr/ppermute | solution.py:130
  2100.8 50.9 %reduce-scatter.16.cloned.1.call-done = f32[192,2304]{1,0:T(8,128)} async-done(((f32[768,2304]{1,0:T(8,128)}), f32[192,2304]{1,0:T(8,128)}) %reduce-scatter.16.cloned.1.call-update) | async-done | bytes 1769488
  2181.8 110.6 %reduce-scatter.14.cloned.1.call-done = bf16[4,6,128,768]{3,2,1,0:T(8,128)(2,1)} async-done(((bf16[4,6,256,768]{3,2,1,0:T(8,128)(2,1)}), bf16[4,6,128,768]{3,2,1,0:T(8,128)(2,1)}) %reduce-scatter.14.cloned.1.call-update) | async-done | bytes 4718608 | tf_op jit(solution)/shard_map/reduce_scatter | solution.py:138
  2292.4 74.7 %reduce-scatter.10.cloned.1.call-done = f32[1,192,3072]{2,1,0:T(8,128)} async-done(((f32[1,768,3072]{2,1,0:T(8,128)}), f32[1,192,3072]{2,1,0:T(8,128)}) %reduce-scatter.10.cloned.1.call-update) | async-done | bytes 2359312 | tf_op jit(solution)/shard_map/reduce_scatter | solution.py:136
  2367.1 74.7 %reduce-scatter.12.cloned.1.call-done = f32[1,768,768]{2,1,0:T(8,128)} async-done(((f32[1,3072,768]{2,1,0:T(8,128)}), f32[1,768,768]{2,1,0:T(8,128)}) %reduce-scatter.12.cloned.1.call-update) | async-done | bytes 2359312 | tf_op jit(solution)/shard_map/reduce_scatter | solution.py:136
  (439 shorter events, 1439.3 us)
Async XLA Ops:
  7.2 59.8 %all-gather.5.cloned.1.call-start = ((), (), s32[]{:S(2)}) async-start(), calls=%async_computation.5 | async-start | bytes 9830400 | tf_op jit(solution)/shard_map/all_gather | solution.py:96
  11.3 71.7 %all-gather.7.cloned.1.call-start = ((), (), s32[]{:S(2)}) async-start(), calls=%async_computation.6 | async-start | bytes 1474560 | tf_op jit(solution)/shard_map/all_gather | solution.py:96
  12.0 107.0 %all-gather.11.cloned.1.call-start = ((), (), s32[]{:S(2)}) async-start(), calls=%async_computation.8 | async-start | bytes 5898240 | tf_op jit(solution)/shard_map/all_gather | solution.py:96
  12.8 142.2 %all-gather.9.cloned.1.call-start = ((), (), s32[]{:S(2)}) async-start(), calls=%async_computation.7 | async-start | bytes 5898240 | tf_op jit(solution)/shard_map/all_gather | solution.py:96
  13.4 2138.4 %reduce-scatter.16.cloned.1.call-start = ((), (), s32[]{:S(2)}) async-start(), calls=%async_computation.13 | async-start | bytes 8847360
  196.7 86.9 %collective-permute-start.1 = (bf16[6,256,768]{2,1,0:T(8,128)(2,1)}, bf16[6,256,768]{2,1,0:T(8,128)(2,1)}, u32[]{:S(2)}, u32[]{:S(2)}) collective-permute-start(bf16[6,256,768]{2,1,0:T(8,128)(2,1)} %get-tuple-element.758), channel_id=1, source_target_pairs={{4,0},{5,1},{6,2},{7,3}} | collective-permute-start | bytes 7077896 | tf_op jit(solution)/shard_map/while/body/eval_jaxpr/ppermute | solution.py:130
  277.1 52.4 %collective-permute-start = (bf16[6,256,768]{2,1,0:T(8,128)(2,1)S(1)}, bf16[6,256,768]{2,1,0:T(8,128)(2,1)}, u32[]{:S(2)}, u32[]{:S(2)}) collective-permute-start(bf16[6,256,768]{2,1,0:T(8,128)(2,1)S(1)} %get-tuple-element.842), channel_id=1, source_target_pairs={{0,4},{1,5},{2,6},{3,7}} | collective-permute-start | bytes 7077896 | tf_op jit(solution)/shard_map/while/body/eval_jaxpr/ppermute | solution.py:129
  344.8 302.5 %collective-permute-start.1 = (bf16[6,256,768]{2,1,0:T(8,128)(2,1)}, bf16[6,256,768]{2,1,0:T(8,128)(2,1)}, u32[]{:S(2)}, u32[]{:S(2)}) collective-permute-start(bf16[6,256,768]{2,1,0:T(8,128)(2,1)} %get-tuple-element.758), channel_id=1, source_target_pairs={{4,0},{5,1},{6,2},{7,3}} | collective-permute-start | bytes 7077896 | tf_op jit(solution)/shard_map/while/body/eval_jaxpr/ppermute | solution.py:130
  425.3 267.3 %collective-permute-start = (bf16[6,256,768]{2,1,0:T(8,128)(2,1)S(1)}, bf16[6,256,768]{2,1,0:T(8,128)(2,1)}, u32[]{:S(2)}, u32[]{:S(2)}) collective-permute-start(bf16[6,256,768]{2,1,0:T(8,128)(2,1)S(1)} %get-tuple-element.842), channel_id=1, source_target_pairs={{0,4},{1,5},{2,6},{3,7}} | collective-permute-start | bytes 7077896 | tf_op jit(solution)/shard_map/while/body/eval_jaxpr/ppermute | solution.py:129
  775.6 44.4 %copy-start.2 = (bf16[6,256,768]{2,1,0:T(8,128)(2,1)}, bf16[6,256,768]{2,1,0:T(8,128)(2,1)S(1)}, u32[]{:S(2)}) copy-start(bf16[6,256,768]{2,1,0:T(8,128)(2,1)S(1)} %bitcast_select_fusion) | copy-start | bytes 7077892 | tf_op jit(solution)/shard_map/while/body/eval_jaxpr/cond
  919.4 91.5 %collective-permute-start.1 = (bf16[6,256,768]{2,1,0:T(8,128)(2,1)}, bf16[6,256,768]{2,1,0:T(8,128)(2,1)}, u32[]{:S(2)}, u32[]{:S(2)}) collective-permute-start(bf16[6,256,768]{2,1,0:T(8,128)(2,1)} %get-tuple-element.758), channel_id=1, source_target_pairs={{4,0},{5,1},{6,2},{7,3}} | collective-permute-start | bytes 7077896 | tf_op jit(solution)/shard_map/while/body/eval_jaxpr/ppermute | solution.py:130
  999.5 55.8 %collective-permute-start = (bf16[6,256,768]{2,1,0:T(8,128)(2,1)S(1)}, bf16[6,256,768]{2,1,0:T(8,128)(2,1)}, u32[]{:S(2)}, u32[]{:S(2)}) collective-permute-start(bf16[6,256,768]{2,1,0:T(8,128)(2,1)S(1)} %get-tuple-element.842), channel_id=1, source_target_pairs={{0,4},{1,5},{2,6},{3,7}} | collective-permute-start | bytes 7077896 | tf_op jit(solution)/shard_map/while/body/eval_jaxpr/ppermute | solution.py:129
  1138.4 44.4 %copy-start.2 = (bf16[6,256,768]{2,1,0:T(8,128)(2,1)}, bf16[6,256,768]{2,1,0:T(8,128)(2,1)S(1)}, u32[]{:S(2)}) copy-start(bf16[6,256,768]{2,1,0:T(8,128)(2,1)S(1)} %bitcast_select_fusion) | copy-start | bytes 7077892 | tf_op jit(solution)/shard_map/while/body/eval_jaxpr/cond
  1281.9 91.5 %collective-permute-start.1 = (bf16[6,256,768]{2,1,0:T(8,128)(2,1)}, bf16[6,256,768]{2,1,0:T(8,128)(2,1)}, u32[]{:S(2)}, u32[]{:S(2)}) collective-permute-start(bf16[6,256,768]{2,1,0:T(8,128)(2,1)} %get-tuple-element.758), channel_id=1, source_target_pairs={{4,0},{5,1},{6,2},{7,3}} | collective-permute-start | bytes 7077896 | tf_op jit(solution)/shard_map/while/body/eval_jaxpr/ppermute | solution.py:130
  1362.2 54.7 %collective-permute-start = (bf16[6,256,768]{2,1,0:T(8,128)(2,1)S(1)}, bf16[6,256,768]{2,1,0:T(8,128)(2,1)}, u32[]{:S(2)}, u32[]{:S(2)}) collective-permute-start(bf16[6,256,768]{2,1,0:T(8,128)(2,1)S(1)} %get-tuple-element.842), channel_id=1, source_target_pairs={{0,4},{1,5},{2,6},{3,7}} | collective-permute-start | bytes 7077896 | tf_op jit(solution)/shard_map/while/body/eval_jaxpr/ppermute | solution.py:129
  1500.2 44.4 %copy-start.2 = (bf16[6,256,768]{2,1,0:T(8,128)(2,1)}, bf16[6,256,768]{2,1,0:T(8,128)(2,1)S(1)}, u32[]{:S(2)}) copy-start(bf16[6,256,768]{2,1,0:T(8,128)(2,1)S(1)} %bitcast_select_fusion) | copy-start | bytes 7077892 | tf_op jit(solution)/shard_map/while/body/eval_jaxpr/cond
  1644.0 91.3 %collective-permute-start.1 = (bf16[6,256,768]{2,1,0:T(8,128)(2,1)}, bf16[6,256,768]{2,1,0:T(8,128)(2,1)}, u32[]{:S(2)}, u32[]{:S(2)}) collective-permute-start(bf16[6,256,768]{2,1,0:T(8,128)(2,1)} %get-tuple-element.758), channel_id=1, source_target_pairs={{4,0},{5,1},{6,2},{7,3}} | collective-permute-start | bytes 7077896 | tf_op jit(solution)/shard_map/while/body/eval_jaxpr/ppermute | solution.py:130
  1653.8 124.1 %collective-permute-start = (bf16[6,256,768]{2,1,0:T(8,128)(2,1)S(1)}, bf16[6,256,768]{2,1,0:T(8,128)(2,1)}, u32[]{:S(2)}, u32[]{:S(2)}) collective-permute-start(bf16[6,256,768]{2,1,0:T(8,128)(2,1)S(1)} %get-tuple-element.842), channel_id=1, source_target_pairs={{0,4},{1,5},{2,6},{3,7}} | collective-permute-start | bytes 7077896 | tf_op jit(solution)/shard_map/while/body/eval_jaxpr/ppermute | solution.py:129
  2004.4 51.4 %collective-permute-start.1 = (bf16[6,256,768]{2,1,0:T(8,128)(2,1)}, bf16[6,256,768]{2,1,0:T(8,128)(2,1)}, u32[]{:S(2)}, u32[]{:S(2)}) collective-permute-start(bf16[6,256,768]{2,1,0:T(8,128)(2,1)} %get-tuple-element.758), channel_id=1, source_target_pairs={{4,0},{5,1},{6,2},{7,3}} | collective-permute-start | bytes 7077896 | tf_op jit(solution)/shard_map/while/body/eval_jaxpr/ppermute | solution.py:130
  2014.6 48.6 %collective-permute-start = (bf16[6,256,768]{2,1,0:T(8,128)(2,1)S(1)}, bf16[6,256,768]{2,1,0:T(8,128)(2,1)}, u32[]{:S(2)}, u32[]{:S(2)}) collective-permute-start(bf16[6,256,768]{2,1,0:T(8,128)(2,1)S(1)} %get-tuple-element.842), channel_id=1, source_target_pairs={{0,4},{1,5},{2,6},{3,7}} | collective-permute-start | bytes 7077896 | tf_op jit(solution)/shard_map/while/body/eval_jaxpr/ppermute | solution.py:129
  2094.4 87.4 %reduce-scatter.8.cloned.1.call-start = ((), (), s32[]{:S(2)}) async-start(), calls=%async_computation.9 | async-start | bytes 2949120 | tf_op jit(solution)/shard_map/reduce_scatter | solution.py:136
  2094.9 197.5 %reduce-scatter.14.cloned.1.call-start = ((), (), s32[]{:S(2)}) async-start(), calls=%async_computation.12 | async-start | bytes 14155776 | tf_op jit(solution)/shard_map/reduce_scatter | solution.py:138
  2099.3 267.8 %reduce-scatter.10.cloned.1.call-start = ((), (), s32[]{:S(2)}) async-start(), calls=%async_computation.10 | async-start | bytes 11796480 | tf_op jit(solution)/shard_map/reduce_scatter | solution.py:136
  2100.1 341.7 %reduce-scatter.12.cloned.1.call-start = ((), (), s32[]{:S(2)}) async-start(), calls=%async_computation.11 | async-start | bytes 11796480 | tf_op jit(solution)/shard_map/reduce_scatter | solution.py:136
  (89 other events, 719.3 us)
Sparse Core Ops, SparseCore 0:
  11.4 55.5 all-gather.4
  68.5 14.4 all-gather.6
  84.5 34.5 all-gather.10
  120.4 34.5 all-gather.8
  2094.5 57.2 reduce-scatter.15
  2154.7 27.0 reduce-scatter.7
  2184.6 107.7 reduce-scatter.13
  2295.5 71.4 reduce-scatter.9
  2370.2 71.4 reduce-scatter.11
where the time goes:
time: 2460 us; the launch traced here: 2450 us
  matrix products  918 us (37%)
  waiting for transfers between devices  730 us (30%)
  starting transfers between devices  324 us (13%)
  other arithmetic  292 us (12%)
  local copies, waits for them, and re-layouts  130 us (5%)
  loops' own time  39.9 us (2%)
    ppermute x6, starting transfers between devices, run_tick(): fwd_buf = lax.ppermute(stage_out, 'pp', fwd_pairs)  316 us
    ppermute x6, waiting for transfers between devices, run_tick(): fwd_buf = lax.ppermute(stage_out, 'pp', fwd_pairs)  229 us
    dot_general x16, matrix products, attn_core(): jnp.einsum('bqnh,bknh->bnqk', q_heads, k_heads, preferred_element_type=jn...  179 us
    sub x8, other arithmetic, attn_core(): jax.nn.softmax(jnp.where(causal, scores, -1e+30), axis=-1)  171 us
    reduce_scatter x3, waiting for transfers between devices, device_step(): lax.psum_scatter(acc_part, 'dp', scatter_dimension=1, tiled=True)  170 us
    dot_general x16, matrix products, attn_core(): jnp.einsum('bnqk,bknh->bqnh', prob_bf, v_heads, preferred_element_type=jn...  141 us
    all_gather x4, waiting for transfers between devices, device_step(): lax.all_gather(w_part, 'dp', axis=1, tiled=True)  130 us
    reduce_scatter x1, waiting for transfers between devices, device_step(): lax.psum_scatter(last_out, 'pp', scatter_dimension=2, tiled=True)  111 us
  transfers between devices with their start and end apart: 21, of which 16 were waited for; matrix products, arithmetic and copies ran while one was open for 15% of the time, Pallas kernels for 0%

commit v1 on v0

v1 whole, which is shorter than its diff:
```python
import functools
import math

import jax
import jax.numpy as jnp
from jax import lax
from jax.experimental import pallas as pl
from jax.experimental.pallas import tpu as pltpu
from jax.sharding import PartitionSpec as P

NORM_EPS = 1e-6
BF = jnp.bfloat16
F32 = jnp.float32
VMEM_LIMIT = 62 * 1024 * 1024
GELU_C = math.sqrt(2.0 / math.pi)
NN = (((1,), (0,)), ((), ()))
NT = (((1,), (1,)), ((), ()))
TN = (((0,), (0,)), ((), ()))


def dot(lhs, rhs, dims=NN):
    return lax.dot_general(lhs, rhs, dims, preferred_element_type=F32)


def rms_scale(hid_f32):
    return lax.rsqrt(jnp.mean(hid_f32 * hid_f32, axis=-1, keepdims=True) + NORM_EPS)


def rms_pull(hid_f32, scale, ct):
    inner = jnp.mean(ct * hid_f32, axis=-1, keepdims=True)
    return scale * (ct - hid_f32 * (scale * scale * inner))


def gelu_parts(pre):
    sq = pre * pre
    th = jnp.tanh(pre * (GELU_C + (GELU_C * 0.044715) * sq))
    half = 0.5 + 0.5 * th
    return sq, th, half


def head_masks(value):
    lane = lax.broadcasted_iota(jnp.int32, (1, 128), 1)
    low = jnp.where(lane < 64, value, 0.0).astype(BF)
    high = jnp.where(lane < 64, 0.0, value).astype(BF)
    return low, high


def causal_tile():
    return lax.broadcasted_iota(jnp.int32, (128, 128), 0) <= lax.broadcasted_iota(jnp.int32, (128, 128), 1)


def attn_fwd_kernel(h_ref, w_ref, qkv_ref, attn_ref, lse_ref):
    d_model = h_ref.shape[-1]
    hid = h_ref[...].astype(F32)
    normed = (hid * rms_scale(hid)).astype(BF)
    for part in range(3):
        cols = slice(part * d_model, (part + 1) * d_model)
        qkv_ref[:, cols] = dot(normed, w_ref[:, cols]).astype(BF)
    masks = head_masks(0.125)
    keep = causal_tile()
    zero_tile = jnp.zeros((128, 128), BF)
    for pair in range(d_model // 128):
        base = pair * 128
        q_pair = qkv_ref[:, base:base + 128]
        k_pair = qkv_ref[:, d_model + base:d_model + base + 128]
        v_tr = qkv_ref[:, 2 * d_model + base:2 * d_model + base + 128].T
        outs = []
        for sub in range(2):
            scores = dot(k_pair, q_pair * masks[sub], NT)
            s00 = jnp.where(keep, scores[:128, :128], -1e30)
            s01 = scores[:128, 128:]
            s11 = jnp.where(keep, scores[128:, 128:], -1e30)
            top0 = jnp.max(s00, axis=0, keepdims=True)
            top1 = jnp.max(jnp.maximum(s01, s11), axis=0, keepdims=True)
            e00 = jnp.exp(s00 - top0)
            e01 = jnp.exp(s01 - top1)
            e11 = jnp.exp(s11 - top1)
            sum0 = jnp.sum(e00, axis=0, keepdims=True)
            sum1 = jnp.sum(e01 + e11, axis=0, keepdims=True)
            inv0 = 1.0 / sum0
            inv1 = 1.0 / sum1
            prob = jnp.concatenate([
                jnp.concatenate([(e00 * inv0).astype(BF), (e01 * inv1).astype(BF)], axis=1),
                jnp.concatenate([zero_tile, (e11 * inv1).astype(BF)], axis=1)], axis=0)
            lse_ref[2 * pair + sub:2 * pair + sub + 1, :] = jnp.concatenate([top0 + jnp.log(sum0), top1 + jnp.log(sum1)], axis=1)
            outs.append(dot(v_tr[sub * 64:(sub + 1) * 64], prob))
        attn_ref[:, base:base + 128] = jnp.concatenate(outs, axis=0).T.astype(BF)


def attn_forward(hidden, w_qkv):
    seqs, seq_len, d_model = hidden.shape
    heads = d_model // 64
    flops = 2 * seqs * seq_len * d_model * 3 * d_model + 8 * seqs * heads * seq_len * seq_len * 128
    return pl.pallas_call(
        attn_fwd_kernel,
        grid=(seqs,),
        in_specs=[
            pl.BlockSpec((None, seq_len, d_model), lambda i: (i, 0, 0)),
            pl.BlockSpec((d_model, 3 * d_model), lambda i: (0, 0), pipeline_mode=pl.Buffered(1)),
        ],
        out_specs=[
            pl.BlockSpec((None, seq_len, 3 * d_model), lambda i: (i, 0, 0)),
            pl.BlockSpec((None, seq_len, d_model), lambda i: (i, 0, 0)),
            pl.BlockSpec((None, heads, seq_len), lambda i: (i, 0, 0)),
        ],
        out_shape=[
            jax.ShapeDtypeStruct((seqs, seq_len, 3 * d_model), BF),
            jax.ShapeDtypeStruct((seqs, seq_len, d_model), BF),
            jax.ShapeDtypeStruct((seqs, heads, seq_len), F32),
        ],
        cost_estimate=pl.CostEstimate(flops=flops, bytes_accessed=40 << 20, transcendentals=0),
        compiler_params=pltpu.CompilerParams(vmem_limit_bytes=VMEM_LIMIT),
        name='attn_fwd',
    )(hidden, w_qkv)


def mlp_fwd_kernel(h_ref, attn_ref, wp_ref, wu_ref, wd_ref, mid_ref, up_ref, out_ref):
    d_model = h_ref.shape[-1]
    mid = (h_ref[...].astype(F32) + dot(attn_ref[...], wp_ref[...])).astype(BF)
    mid_ref[...] = mid
    mid = mid.astype(F32)
    normed = (mid * rms_scale(mid)).astype(BF)
    total = mid
    for part in range(wu_ref.shape[1] // d_model):
        cols = slice(part * d_model, (part + 1) * d_model)
        up = dot(normed, wu_ref[:, cols]).astype(BF)
        up_ref[:, cols] = up
        pre = up.astype(F32)
        act = (pre * gelu_parts(pre)[2]).astype(BF)
        total = total + dot(act, wd_ref[cols, :])
    out_ref[...] = total.astype(BF)


def mlp_forward(hidden, attn, w_proj, w_up, w_down, rows=512):
    tokens, d_model = hidden.shape
    d_ff = w_up.shape[1]
    flops = 2 * tokens * d_model * (d_model + 2 * d_ff)
    row_spec = pl.BlockSpec((rows, d_model), lambda i: (i, 0))
    whole = lambda shape: pl.BlockSpec(shape, lambda i: (0, 0), pipeline_mode=pl.Buffered(1))
    return pl.pallas_call(
        mlp_fwd_kernel,
        grid=(tokens // rows,),
        in_specs=[row_spec, row_spec, whole(w_proj.shape), whole(w_up.shape), whole(w_down.shape)],
        out_specs=[row_spec, pl.BlockSpec((rows, d_ff), lambda i: (i, 0)), row_spec],
        out_shape=[
            jax.ShapeDtypeStruct((tokens, d_model), BF),
            jax.ShapeDtypeStruct((tokens, d_ff), BF),
            jax.ShapeDtypeStruct((tokens, d_model), BF),
        ],
        cost_estimate=pl.CostEstimate(flops=flops, bytes_accessed=50 << 20, transcendentals=0),
        compiler_params=pltpu.CompilerParams(vmem_limit_bytes=VMEM_LIMIT),
        name='mlp_fwd',
    )(hidden, attn, w_proj, w_up, w_down)


def mlp_bwd_kernel(ct_ref, up_ref, mid_ref, attn_ref, wp_ref, wu_ref, wd_ref,
                   ct_mid_ref, ct_attn_ref, gd_out, gu_out, gp_out, gd_acc, gu_acc, gp_acc, sems):
    step = pl.program_id(0)
    last = pl.num_programs(0) - 1
    d_model = ct_ref.shape[-1]
    parts = wu_ref.shape[1] // d_model

    @pl.when(step == 0)
    def _():
        gd_acc[...] = jnp.zeros_like(gd_acc)
        gu_acc[...] = jnp.zeros_like(gu_acc)
        gp_acc[...] = jnp.zeros_like(gp_acc)

    def down_copy(part):
        sl = pl.ds(part * d_model, d_model)
        return pltpu.make_async_copy(gd_acc.at[sl, :], gd_out.at[sl, :], sems.at[part])

    def up_copy(part):
        sl = pl.ds(part * d_model, d_model)
        return pltpu.make_async_copy(gu_acc.at[:, sl], gu_out.at[:, sl], sems.at[parts + part])

    proj_copy = pltpu.make_async_copy(gp_acc, gp_out, sems.at[2 * parts])

    ct = ct_ref[...]
    mid = mid_ref[...].astype(F32)
    scale = rms_scale(mid)
    normed = (mid * scale).astype(BF)
    ct_norm = jnp.zeros(mid.shape, F32)
    for part in range(parts):
        cols = slice(part * d_model, (part + 1) * d_model)
        pre = up_ref[:, cols].astype(F32)
        sq, th, half = gelu_parts(pre)
        act = (pre * half).astype(BF)
        slope = half + (0.5 * pre) * (1.0 - th * th) * (GELU_C + (3.0 * 0.044715 * GELU_C) * sq)
        gd_acc[cols, :] += dot(act, ct, TN)
        ct_act = dot(ct, wd_ref[cols, :], NT).astype(BF).astype(F32)
        ct_up = (ct_act * slope).astype(BF)
        gu_acc[:, cols] += dot(normed, ct_up, TN)
        ct_norm = ct_norm + dot(ct_up, wu_ref[:, cols], NT)

        @pl.when(step == last)
        def _():
            down_copy(part).start()
            up_copy(part).start()

    ct_norm = ct_norm.astype(BF).astype(F32)
    ct_mid = (ct.astype(F32) + rms_pull(mid, scale, ct_norm)).astype(BF)
    ct_mid_ref[...] = ct_mid
    gp_acc[...] += dot(attn_ref[...], ct_mid, TN)
    ct_attn_ref[...] = dot(ct_mid, wp_ref[...], NT).astype(BF)

    @pl.when(step == last)
    def _():
        proj_copy.start()
        for part in range(parts):
            down_copy(part).wait()
            up_copy(part).wait()
        proj_copy.wait()


def mlp_backward(ct, up, mid, attn, w_proj, w_up, w_down, rows=512):
    tokens, d_model = ct.shape
    d_ff = w_up.shape[1]
    parts = d_ff // d_model
    flops = 4 * tokens * d_model * (d_model + 2 * d_ff)
    row_spec = pl.BlockSpec((rows, d_model), lambda i: (i, 0))
    whole = lambda shape: pl.BlockSpec(shape, lambda i: (0, 0), pipeline_mode=pl.Buffered(1))
    hbm = pl.BlockSpec(memory_space=pl.ANY)
    return pl.pallas_call(
        mlp_bwd_kernel,
        grid=(tokens // rows,),
        in_specs=[row_spec, pl.BlockSpec((rows, d_ff), lambda i: (i, 0)), row_spec, row_spec,
                  whole(w_proj.shape), whole(w_up.shape), whole(w_down.shape)],
        out_specs=[row_spec, row_spec, hbm, hbm, hbm],
        out_shape=[
            jax.ShapeDtypeStruct((tokens, d_model), BF),
            jax.ShapeDtypeStruct((tokens, d_model), BF),
            jax.ShapeDtypeStruct((d_ff, d_model), F32),
            jax.ShapeDtypeStruct((d_model, d_ff), F32),
            jax.ShapeDtypeStruct((d_model, d_model), F32),
        ],
        scratch_shapes=[
            pltpu.VMEM((d_ff, d_model), F32),
            pltpu.VMEM((d_model, d_ff), F32),
            pltpu.VMEM((d_model, d_model), F32),
            pltpu.SemaphoreType.DMA((2 * parts + 1,)),
        ],
        cost_estimate=pl.CostEstimate(flops=flops, bytes_accessed=70 << 20, transcendentals=0),
        compiler_params=pltpu.CompilerParams(vmem_limit_bytes=VMEM_LIMIT),
        name='mlp_bwd',
    )(ct, up, mid, attn, w_proj, w_up, w_down)


def attn_bwd_kernel(with_input, *refs):
    if with_input:
        h_ref, qkv_ref, lse_ref, ct_attn_ref, ct_mid_ref, w_ref, ct_h_ref, g_out, dqkv, g_acc, sem = refs
    else:
        h_ref, qkv_ref, lse_ref, ct_attn_ref, g_out, dqkv, g_acc, sem = refs
    step = pl.program_id(0)
    last = pl.num_programs(0) - 1
    d_model = h_ref.shape[-1]

    @pl.when(step == 0)
    def _():
        g_acc[...] = jnp.zeros_like(g_acc)

    q_masks = head_masks(0.125)
    o_masks = head_masks(1.0)
    keep = causal_tile()
    zero_tile = jnp.zeros((128, 128), BF)

    def square(t00, t01, t11):
        return jnp.concatenate([
            jnp.concatenate([t00.astype(BF), t01.astype(BF)], axis=1),
            jnp.concatenate([zero_tile, t11.astype(BF)], axis=1)], axis=0)

    for pair in range(d_model // 128):
        base = pair * 128
        q_pair = qkv_ref[:, base:base + 128]
        k_pair = qkv_ref[:, d_model + base:d_model + base + 128]
        v_pair = qkv_ref[:, 2 * d_model + base:2 * d_model + base + 128]
        o_pair = ct_attn_ref[:, base:base + 128]
        k_tr = k_pair.T
        dq_parts = []
        dk_pair = None
        dv_pair = None
        for sub in range(2):
            q_sub = q_pair * q_masks[sub]
            o_sub = o_pair * o_masks[sub]
            scores = dot(k_pair, q_sub, NT)
            d_prob = dot(v_pair, o_sub, NT)
            lse0 = lse_ref[2 * pair + sub:2 * pair + sub + 1, :128]
            lse1 = lse_ref[2 * pair + sub:2 * pair + sub + 1, 128:]
            p00 = jnp.exp(jnp.where(keep, scores[:128, :128] - lse0, -1e30))
            p01 = jnp.exp(scores[:128, 128:] - lse1)
            p11 = jnp.exp(jnp.where(keep, scores[128:, 128:] - lse1, -1e30))
            d00 = d_prob[:128, :128].astype(BF).astype(F32)
            d01 = d_prob[:128, 128:].astype(BF).astype(F32)
            d11 = d_prob[128:, 128:].astype(BF).astype(F32)
            m0 = jnp.sum(p00 * d00, axis=0, keepdims=True)
            m1 = jnp.sum(p01 * d01 + p11 * d11, axis=0, keepdims=True)
            prob = square(p00, p01, p11)
            d_score = square(p00 * (d00 - m0), p01 * (d01 - m1), p11 * (d11 - m1))
            dv_sub = dot(prob, o_sub)
            dk_sub = dot(d_score, q_sub)
            dv_pair = dv_sub if dv_pair is None else dv_pair + dv_sub
            dk_pair = dk_sub if dk_pair is None else dk_pair + dk_sub
            dq_parts.append(dot(k_tr[sub * 64:(sub + 1) * 64], d_score))
        dqkv[:, base:base + 128] = (jnp.concatenate(dq_parts, axis=0).T * 0.125).astype(BF)
        dqkv[:, d_model + base:d_model + base + 128] = dk_pair.astype(BF)
        dqkv[:, 2 * d_model + base:2 * d_model + base + 128] = dv_pair.astype(BF)

    hid = h_ref[...].astype(F32)
    scale = rms_scale(hid)
    normed = (hid * scale).astype(BF)
    for part in range(3):
        cols = slice(part * d_model, (part + 1) * d_model)
        g_acc[:, cols] += dot(normed, dqkv[:, cols], TN)
    if with_input:
        ct_norm = dot(dqkv[...], w_ref[...], NT).astype(BF).astype(F32)
        ct_h_ref[...] = (ct_mid_ref[...].astype(F32) + rms_pull(hid, scale, ct_norm)).astype(BF)

    @pl.when(step == last)
    def _():
        copy = pltpu.make_async_copy(g_acc, g_out, sem)
        copy.start()
        copy.wait()


def attn_backward(hidden, qkv, lse, ct_attn, ct_mid, w_qkv, with_input):
    seqs, seq_len, d_model = hidden.shape
    heads = d_model // 64
    flops = (4 if with_input else 2) * seqs * seq_len * d_model * 3 * d_model + 20 * seqs * heads * seq_len * seq_len * 128
    row_spec = pl.BlockSpec((None, seq_len, d_model), lambda i: (i, 0, 0))
    in_specs = [row_spec, pl.BlockSpec((None, seq_len, 3 * d_model), lambda i: (i, 0, 0)),
                pl.BlockSpec((None, heads, seq_len), lambda i: (i, 0, 0)), row_spec]
    args = [hidden, qkv, lse, ct_attn]
    out_specs = [pl.BlockSpec(memory_space=pl.ANY)]
    out_shape = [jax.ShapeDtypeStruct((d_model, 3 * d_model), F32)]
    if with_input:
        in_specs += [row_spec, pl.BlockSpec((d_model, 3 * d_model), lambda i: (0, 0), pipeline_mode=pl.Buffered(1))]
        args += [ct_mid, w_qkv]
        out_specs = [row_spec] + out_specs
        out_shape = [jax.ShapeDtypeStruct((seqs, seq_len, d_model), BF)] + out_shape
    return pl.pallas_call(
        functools.partial(attn_bwd_kernel, with_input),
        grid=(seqs,),
        in_specs=in_specs,
        out_specs=out_specs,
        out_shape=out_shape,
        scratch_shapes=[
            pltpu.VMEM((seq_len, 3 * d_model), BF),
            pltpu.VMEM((d_model, 3 * d_model), F32),
            pltpu.SemaphoreType.DMA,
        ],
        cost_estimate=pl.CostEstimate(flops=flops, bytes_accessed=50 << 20, transcendentals=0),
        compiler_params=pltpu.CompilerParams(vmem_limit_bytes=VMEM_LIMIT),
        name='attn_bwd_in' if with_input else 'attn_bwd_first',
    )(*args)


def solution(mesh):
    stages = mesh.shape['pp']
    both = ('dp', 'pp')

    def device_step(act_in, loss_seed, w_qkv, w_proj, w_up, w_down):
        stage = lax.axis_index('pp')
        micro = act_in.shape[0] // stages
        seq_len, d_model = act_in.shape[2:]
        seqs = micro * act_in.shape[1]
        tokens = seqs * seq_len
        parts = (w_qkv.reshape(w_qkv.shape[1], -1), w_proj[0], w_up[0], w_down[0])

        layer_shards = ([], [])
        for part in parts:
            half = part.shape[0] // 2
            kept = lax.dynamic_slice_in_dim(part, stage * half, half, 0)
            sent = lax.dynamic_slice_in_dim(part, (1 - stage) * half, half, 0)
            got = lax.ppermute(sent, 'pp', [(0, 1), (1, 0)])
            layer_shards[0].append(jnp.where(stage == 0, kept, got))
            layer_shards[1].append(jnp.where(stage == 0, got, kept))
        weights = [[lax.all_gather(shard, both, axis=0, tiled=True) for shard in shards] for shards in layer_shards]

        hidden = lax.dynamic_slice_in_dim(act_in, stage * micro, micro, 0).reshape(seqs, seq_len, d_model)
        ct = lax.dynamic_slice_in_dim(loss_seed, stage * micro, micro, 0).reshape(tokens, d_model)

        saved = []
        for layer in range(2):
            wq, wp, wu, wd = weights[layer]
            qkv, attn, lse = attn_forward(hidden, wq)
            attn = attn.reshape(tokens, d_model)
            mid, up, out = mlp_forward(hidden.reshape(tokens, d_model), attn, wp, wu, wd)
            saved.append((hidden, qkv, attn, lse, mid, up))
            hidden = out.reshape(seqs, seq_len, d_model)

        half_len = seq_len // 2
        final = hidden.reshape(micro, act_in.shape[1], seq_len, d_model)
        kept = lax.dynamic_slice_in_dim(final, stage * half_len, half_len, 2)
        sent = lax.dynamic_slice_in_dim(final, (1 - stage) * half_len, half_len, 2)
        got = lax.ppermute(sent, 'pp', [(0, 1), (1, 0)])
        act_out = jnp.where(stage == 0, jnp.concatenate([kept, got]), jnp.concatenate([got, kept]))

        def reduce_rows(grad, layer):
            block = lax.psum_scatter(grad, both, scatter_dimension=0, tiled=True)
            got = lax.ppermute(block, 'pp', [(1 - layer, layer)])
            return jnp.concatenate([block, got] if layer == 0 else [got, block])

        reduced = [None, None]
        for layer in (1, 0):
            wq, wp, wu, wd = weights[layer]
            hid, qkv, attn, lse, mid, up = saved[layer]
            ct_mid, ct_attn, gd, gu, gp = mlp_backward(ct, up, mid, attn, wp, wu, wd)
            shape3 = (seqs, seq_len, d_model)
            res = attn_backward(hid, qkv, lse, ct_attn.reshape(shape3), ct_mid.reshape(shape3), wq, layer > 0)
            gq = res[-1]
            ct = res[0].reshape(tokens, d_model) if layer > 0 else None
            reduced[layer] = [reduce_rows(grad, layer) for grad in (gd, gu, gp, gq)]
        gd, gu, gp, gq = [jnp.where(stage == 0, first, second) for first, second in zip(*reduced)]
        return gq.reshape(w_qkv.shape), gp[None], gu[None], gd[None], act_out

    weight_spec = P('pp', 'dp')
    act_spec = P(None, 'dp')
    return jax.shard_map(device_step, mesh=mesh, in_specs=(act_spec, act_spec, weight_spec, weight_spec, weight_spec, weight_spec), out_specs=(weight_spec, weight_spec, weight_spec, weight_spec, P(None, 'dp', 'pp')), check_vma=False)
```

time: 2460 us -> 1220 us (0.50)
  matrix products: 918 us -> 0 us
  Pallas kernels: 0 us -> 549 us
  starting transfers between devices: 324 us -> 33.8 us
  other arithmetic: 292 us -> 22.8 us
  waiting for transfers between devices: 730 us -> 580 us
  local copies, waits for them, and re-layouts: 130 us -> 21.3 us
  loops' own time: 39.9 us -> 0 us
    dot_general x88 -> x0, matrix products: 918 us -> none  [the longest x16 179 us: attn_core(): jnp.einsum('bqnh,bknh->bnqk', q_heads, k_heads, preferred_element_type=jn...]
    pallas_call x0 -> x8, Pallas kernels: none -> 549 us  [the longest x2 198 us: mlp_backward(): pl.pallas_call(mlp_bwd_kernel, grid=(tokens // rows,), in_specs=[row_spec...]
    ppermute x12 -> x13, starting transfers between devices: 324 us -> 33.2 us  [the longest x8 22.4 us: reduce_rows(): got = lax.ppermute(block, 'pp', [(1 - layer, layer)])]
    ppermute x12 -> x13, waiting for transfers between devices: 264 us -> 51.6 us  [the longest x5 47.9 us: device_step(): got = lax.ppermute(sent, 'pp', [(0, 1), (1, 0)])]
    reduce_scatter x4 -> x8, waiting for transfers between devices: 281 us -> 492 us  [reduce_rows(): block = lax.psum_scatter(grad, both, scatter_dimension=0, tiled=True)]
    sub x8 -> x0, other arithmetic: 171 us -> none  [attn_core(): jax.nn.softmax(jnp.where(causal, scores, -1e+30), axis=-1)]
    all_gather x4 -> x8, waiting for transfers between devices: 130 us -> 30.5 us  [device_step(): lax.all_gather(shard, both, axis=0, tiled=True)]
    unnamed x10 -> x16, waiting for transfers between devices: 54.8 us -> 6.54 us
  transfers between devices with their start and end apart: 21 -> 29, of which waited for: 16 -> 15; matrix products, arithmetic and copies ran while one was open for 15% -> 3% of each run, Pallas kernels for 0% -> 13%
where the time goes in v1:
time: 1220 us
  waiting for transfers between devices  580 us (48%)
  Pallas kernels  549 us (45%)
  starting transfers between devices  33.8 us (3%)
  other arithmetic  22.8 us (2%)
  local copies, waits for them, and re-layouts  21.3 us (2%)
  between operations  14.5 us (1%)
    reduce_scatter x8, waiting for transfers between devices, reduce_rows(): block = lax.psum_scatter(grad, both, scatter_dimension=0, tiled=True)  492 us
    pallas_call x2, Pallas kernels, mlp_backward(): pl.pallas_call(mlp_bwd_kernel, grid=(tokens // rows,), in_specs=[row_spec...  198 us
    pallas_call x2, Pallas kernels, attn_backward(): pl.pallas_call(functools.partial(attn_bwd_kernel, with_input), grid=(seqs...  145 us
    pallas_call x2, Pallas kernels, attn_forward(): pl.pallas_call(attn_fwd_kernel, grid=(seqs,), in_specs=[pl.BlockSpec((Non...  118 us
    pallas_call x2, Pallas kernels, mlp_forward(): pl.pallas_call(mlp_fwd_kernel, grid=(tokens // rows,), in_specs=[row_spec...  88.4 us
    ppermute x5, waiting for transfers between devices, device_step(): got = lax.ppermute(sent, 'pp', [(0, 1), (1, 0)])  47.9 us
    all_gather x8, waiting for transfers between devices, device_step(): lax.all_gather(shard, both, axis=0, tiled=True)  30.5 us
  transfers between devices with their start and end apart: 29, of which 15 were waited for; matrix products, arithmetic and copies ran while one was open for 3% of the time, Pallas kernels for 13%

profile of v1, /device:TPU:0, one launch (start us, length us, event | category | flops | bytes accessed | tf_op | source)
XLA Modules:
  0.0 1221.6 jit_solution(8318437901511618008)
XLA Ops:
  13.2 9.9 collective-permute-done
  32.1 19.4 %collective-permute-done.2 = bf16[96,3072]{1,0:T(8,128)(2,1)S(1)} collective-permute-done((bf16[96,3072]{1,0:T(8,128)(2,1)S(1)}, bf16[96,3072]{1,0:T(8,128)(2,1)S(1)}, u32[]{:S(2)}, u32[]{:S(2)}) %collective-permute-start.2) | collective-permute-done | bytes 589856 | tf_op jit(solution)/shard_map/ppermute | solution.py:374
  55.4 15.1 %collective-permute-done.3 = bf16[384,768]{1,0:T(8,128)(2,1)S(1)} collective-permute-done((bf16[384,768]{1,0:T(8,128)(2,1)S(1)}, bf16[384,768]{1,0:T(8,128)(2,1)S(1)}, u32[]{:S(2)}, u32[]{:S(2)}) %collective-permute-start.3) | collective-permute-done | bytes 589856 | tf_op jit(solution)/shard_map/ppermute | solution.py:374
  74.5 4.8 constant_dynamic-slice_fusion.5
  79.3 4.8 constant_dynamic-slice_fusion.2
  84.1 58.9 %attn_fwd.2 = (bf16[12,256,2304]{2,1,0:T(8,128)(2,1)}, bf16[12,256,768]{2,1,0:T(8,128)(2,1)}, f32[12,12,256]{2,1,0:T(8,128)}) custom-call(bf16[12,256,768]{2,1,0:T(8,128)(2,1)} %bitcast.48, bf16[768,2304]{1,0:T(8,128)(2,1)} %all-gather.9.cloned.1.call-done.w_ref), custom_call_target="tpu_custom_call" | custom-call | flops 20535312384 | bytes 41943040 | tf_op jit(solution)/shard_map/attn_fwd/pallas_call | solution.py:94
  143.0 13.0 %all-gather.15.cloned.1.call-done.wd_ref = bf16[3072,768]{1,0:T(8,128)(2,1)} async-done(((bf16[384,768]{1,0:T(8,128)(2,1)}), bf16[3072,768]{1,0:T(8,128)(2,1)}) %all-gather.15.cloned.1.call-update) | async-done | bytes 4718608 | tf_op jit(solution)/shard_map/all_gather | solution.py:377
  156.0 44.1 %mlp_fwd.2 = (bf16[3072,768]{1,0:T(8,128)(2,1)}, bf16[3072,3072]{1,0:T(8,128)(2,1)}, bf16[3072,768]{1,0:T(8,128)(2,1)}) custom-call(bf16[3072,768]{1,0:T(8,128)(2,1)} %bitcast.49, bf16[3072,768]{1,0:T(8,128)(2,1)} %bitcast.60, bf16[768,768]{1,0:T(8,128)(2,1)} %all-gather.11.cloned.1.call-done.wp_ref, bf16[768,3072]{1,0:T(8,128)(2,1)} %all-gather.13.cloned.1.call-done.wu_ref, ...), custom_call_target="tpu_custom_call" | custom-call | flops 32614907904 | bytes 52428800 | tf_op jit(solution)/shard_map/mlp_fwd/pallas_call | solution.py:140
  200.1 58.7 %attn_fwd.3 = (bf16[12,256,2304]{2,1,0:T(8,128)(2,1)}, bf16[12,256,768]{2,1,0:T(8,128)(2,1)}, f32[12,12,256]{2,1,0:T(8,128)}) custom-call(bf16[12,256,768]{2,1,0:T(8,128)(2,1)} %bitcast.62, bf16[768,2304]{1,0:T(8,128)(2,1)} %all-gather.17.cloned.1.call-done.w_ref.refs_5_), custom_call_target="tpu_custom_call" | custom-call | flops 20535312384 | bytes 41943040 | tf_op jit(solution)/shard_map/attn_fwd/pallas_call | solution.py:94
  258.9 17.5 %all-gather.23.cloned.1.call-done.wd_ref = bf16[3072,768]{1,0:T(8,128)(2,1)} async-done(((bf16[384,768]{1,0:T(8,128)(2,1)}), bf16[3072,768]{1,0:T(8,128)(2,1)}) %all-gather.23.cloned.1.call-update) | async-done | bytes 4718608 | tf_op jit(solution)/shard_map/all_gather | solution.py:377
  276.3 44.3 %mlp_fwd.3 = (bf16[3072,768]{1,0:T(8,128)(2,1)}, bf16[3072,3072]{1,0:T(8,128)(2,1)}, bf16[3072,768]{1,0:T(8,128)(2,1)}) custom-call(bf16[3072,768]{1,0:T(8,128)(2,1)} %get-tuple-element.31.h_ref, bf16[3072,768]{1,0:T(8,128)(2,1)} %bitcast.64, bf16[768,768]{1,0:T(8,128)(2,1)} %all-gather.19.cloned.1.call-done.wp_ref, ...), custom_call_target="tpu_custom_call" | custom-call | flops 32614907904 | bytes 52428800 | tf_op jit(solution)/shard_map/mlp_fwd/pallas_call | solution.py:140
  320.6 98.7 %mlp_bwd.2 = (bf16[3072,768]{1,0:T(8,128)(2,1)}, bf16[3072,768]{1,0:T(8,128)(2,1)}, f32[3072,768]{1,0:T(8,128)}, f32[768,3072]{1,0:T(8,128)}, f32[768,768]{1,0:T(8,128)}) custom-call(bf16[3072,768]{1,0:T(8,128)(2,1)} %bitcast.51, bf16[3072,3072]{1,0:T(8,128)(2,1)} %get-tuple-element.35.up_ref, bf16[3072,768]{1,0:T(8,128)(2,1)} %get-tuple-element.36.mid_ref, ...), custom_call_target="tpu_custom_call" | custom-call | flops 65229815808 | bytes 73400320 | tf_op jit(solution)/shard_map/mlp_bwd/pallas_call | solution.py:224
  419.3 79.8 %attn_bwd_in.1 = (bf16[12,256,768]{2,1,0:T(8,128)(2,1)}, f32[768,2304]{1,0:T(8,128)}) custom-call(bf16[12,256,768]{2,1,0:T(8,128)(2,1)} %bitcast.63, bf16[12,256,2304]{2,1,0:T(8,128)(2,1)} %get-tuple-element.32.refs_1_, f32[12,12,256]{2,1,0:T(8,128)} %get-tuple-element.33.refs_2_, bf16[12,256,768]{2,1,0:T(8,128)(2,1)} %bitcast.68, ...), custom_call_target="tpu_custom_call" | custom-call | flops 45902462976 | bytes 52428800 | tf_op jit(solution)/shard_map/attn_bwd_in/pallas_call | solution.py:340
  499.1 99.0 %mlp_bwd.3 = (bf16[3072,768]{1,0:T(8,128)(2,1)}, bf16[3072,768]{1,0:T(8,128)(2,1)}, f32[3072,768]{1,0:T(8,128)}, f32[768,3072]{1,0:T(8,128)}, f32[768,768]{1,0:T(8,128)}) custom-call(bf16[3072,768]{1,0:T(8,128)(2,1)} %bitcast.66, bf16[3072,3072]{1,0:T(8,128)(2,1)} %get-tuple-element.40.up_ref, bf16[3072,768]{1,0:T(8,128)(2,1)} %get-tuple-element.41.mid_ref, ...), custom_call_target="tpu_custom_call" | custom-call | flops 65229815808 | bytes 73400320 | tf_op jit(solution)/shard_map/mlp_bwd/pallas_call | solution.py:224
  598.0 65.3 %attn_bwd_first.1 = f32[768,2304]{1,0:T(8,128)} custom-call(bf16[12,256,768]{2,1,0:T(8,128)(2,1)} %bitcast.50, bf16[12,256,2304]{2,1,0:T(8,128)(2,1)} %get-tuple-element.28.refs_1_, f32[12,12,256]{2,1,0:T(8,128)} %get-tuple-element.29.refs_2_, bf16[12,256,768]{2,1,0:T(8,128)(2,1)} %bitcast.69), custom_call_target="tpu_custom_call" | custom-call | flops 35030827008 | bytes 52428800 | tf_op jit(solution)/shard_map/attn_bwd_first/pallas_call | solution.py:340
  673.3 75.8 %reduce-scatter.9.cloned.1.call-done = f32[96,2304]{1,0:T(8,128)} async-done(((f32[768,2304]{1,0:T(8,128)}), f32[96,2304]{1,0:T(8,128)}) %reduce-scatter.9.cloned.1.call-update) | async-done | bytes 884752 | tf_op jit(solution)/shard_map/reduce_scatter | solution.py:399
  750.4 38.6 %reduce-scatter.13.cloned.1.call-done = f32[96,768]{1,0:T(8,128)} async-done(((f32[768,768]{1,0:T(8,128)}), f32[96,768]{1,0:T(8,128)}) %reduce-scatter.13.cloned.1.call-update) | async-done | bytes 294928 | tf_op jit(solution)/shard_map/reduce_scatter | solution.py:399
  790.2 36.4 %reduce-scatter.15.cloned.1.call-done = f32[96,768]{1,0:T(8,128)} async-done(((f32[768,768]{1,0:T(8,128)}), f32[96,768]{1,0:T(8,128)}) %reduce-scatter.15.cloned.1.call-update) | async-done | bytes 294928 | tf_op jit(solution)/shard_map/reduce_scatter | solution.py:399
  830.8 66.7 %reduce-scatter.21.cloned.1.call-done = f32[384,768]{1,0:T(8,128)} async-done(((f32[3072,768]{1,0:T(8,128)}), f32[384,768]{1,0:T(8,128)}) %reduce-scatter.21.cloned.1.call-update) | async-done | bytes 1179664 | tf_op jit(solution)/shard_map/reduce_scatter | solution.py:399
  898.7 73.5 %reduce-scatter.23.cloned.1.call-done = f32[384,768]{1,0:T(8,128)} async-done(((f32[3072,768]{1,0:T(8,128)}), f32[384,768]{1,0:T(8,128)}) %reduce-scatter.23.cloned.1.call-update) | async-done | bytes 1179664 | tf_op jit(solution)/shard_map/reduce_scatter | solution.py:399
  976.6 61.0 %reduce-scatter.11.cloned.1.call-done = f32[96,2304]{1,0:T(8,128)} async-done(((f32[768,2304]{1,0:T(8,128)}), f32[96,2304]{1,0:T(8,128)}) %reduce-scatter.11.cloned.1.call-update) | async-done | bytes 884752 | tf_op jit(solution)/shard_map/reduce_scatter | solution.py:399
  1042.0 66.4 %reduce-scatter.17.cloned.1.call-done = f32[96,3072]{1,0:T(8,128)} async-done(((f32[768,3072]{1,0:T(8,128)}), f32[96,3072]{1,0:T(8,128)}) %reduce-scatter.17.cloned.1.call-update) | async-done | bytes 1179664 | tf_op jit(solution)/shard_map/reduce_scatter | solution.py:399
  1109.7 73.5 %reduce-scatter.19.cloned.1.call-done = f32[96,3072]{1,0:T(8,128)} async-done(((f32[768,3072]{1,0:T(8,128)}), f32[96,3072]{1,0:T(8,128)}) %reduce-scatter.19.cloned.1.call-update) | async-done | bytes 1179664 | tf_op jit(solution)/shard_map/reduce_scatter | solution.py:399
  1187.6 5.7 maximum_select_fusion
  (106 shorter events, 76.3 us)
Async XLA Ops:
  7.2 76.9 %all-gather.9.cloned.1.call-start = ((), (), s32[]{:S(2)}) async-start(), calls=%async_computation.8 | async-start | bytes 3981312 | tf_op jit(solution)/shard_map/all_gather | solution.py:377
  24.1 118.8 %all-gather.11.cloned.1.call-start = ((), (), s32[]{:S(2)}) async-start(), calls=%async_computation.9 | async-start | bytes 1327104 | tf_op jit(solution)/shard_map/all_gather | solution.py:377
  30.2 112.8 %all-gather.13.cloned.1.call-start = ((), (), s32[]{:S(2)}) async-start(), calls=%async_computation.10 | async-start | bytes 5308416 | tf_op jit(solution)/shard_map/all_gather | solution.py:377
  52.8 103.2 %all-gather.15.cloned.1.call-start = ((), (), s32[]{:S(2)}) async-start(), calls=%async_computation.11 | async-start | bytes 5308416 | tf_op jit(solution)/shard_map/all_gather | solution.py:377
  71.8 128.3 %all-gather.17.cloned.1.call-start = ((), (), s32[]{:S(2)}) async-start(), calls=%async_computation.12 | async-start | bytes 3981312 | tf_op jit(solution)/shard_map/all_gather | solution.py:377
  72.4 186.5 %all-gather.19.cloned.1.call-start = ((), (), s32[]{:S(2)}) async-start(), calls=%async_computation.13 | async-start | bytes 1327104 | tf_op jit(solution)/shard_map/all_gather | solution.py:377
  72.9 185.9 %all-gather.21.cloned.1.call-start = ((), (), s32[]{:S(2)}) async-start(), calls=%async_computation.14 | async-start | bytes 5308416 | tf_op jit(solution)/shard_map/all_gather | solution.py:377
  73.7 202.6 %all-gather.23.cloned.1.call-start = ((), (), s32[]{:S(2)}) async-start(), calls=%async_computation.15 | async-start | bytes 5308416 | tf_op jit(solution)/shard_map/all_gather | solution.py:377
  74.4 674.6 %reduce-scatter.9.cloned.1.call-start = ((), (), s32[]{:S(2)}) async-start(), calls=%async_computation.16 | async-start | bytes 7962624 | tf_op jit(solution)/shard_map/reduce_scatter | solution.py:399
  663.3 125.6 %reduce-scatter.13.cloned.1.call-start = ((), (), s32[]{:S(2)}) async-start(), calls=%async_computation.18 | async-start | bytes 2654208 | tf_op jit(solution)/shard_map/reduce_scatter | solution.py:399
  663.9 162.7 %reduce-scatter.15.cloned.1.call-start = ((), (), s32[]{:S(2)}) async-start(), calls=%async_computation.19 | async-start | bytes 2654208 | tf_op jit(solution)/shard_map/reduce_scatter | solution.py:399
  664.7 232.7 %reduce-scatter.21.cloned.1.call-start = ((), (), s32[]{:S(2)}) async-start(), calls=%async_computation.22 | async-start | bytes 10616832 | tf_op jit(solution)/shard_map/reduce_scatter | solution.py:399
  665.2 307.0 %reduce-scatter.23.cloned.1.call-start = ((), (), s32[]{:S(2)}) async-start(), calls=%async_computation.23 | async-start | bytes 10616832 | tf_op jit(solution)/shard_map/reduce_scatter | solution.py:399
  666.0 371.6 %reduce-scatter.11.cloned.1.call-start = ((), (), s32[]{:S(2)}) async-start(), calls=%async_computation.17 | async-start | bytes 7962624 | tf_op jit(solution)/shard_map/reduce_scatter | solution.py:399
  666.6 441.8 %reduce-scatter.17.cloned.1.call-start = ((), (), s32[]{:S(2)}) async-start(), calls=%async_computation.20 | async-start | bytes 10616832 | tf_op jit(solution)/shard_map/reduce_scatter | solution.py:399
  667.2 516.0 %reduce-scatter.19.cloned.1.call-start = ((), (), s32[]{:S(2)}) async-start(), calls=%async_computation.21 | async-start | bytes 10616832 | tf_op jit(solution)/shard_map/reduce_scatter | solution.py:399
  671.9 226.8 %collective-permute-start.12 = (bf16[2,6,128,768]{3,2,1,0:T(8,128)(2,1)}, bf16[2,6,128,768]{3,2,1,0:T(8,128)(2,1)}, u32[]{:S(2)}, u32[]{:S(2)}) collective-permute-start(bf16[2,6,128,768]{3,2,1,0:T(8,128)(2,1)} %get-tuple-element.52), channel_id=1, source_target_pairs={{0,4},{4,0},{1,5},{5,1},{2,6},{6,2},{3,7},{7,3}} | collective-permute-start | bytes 7077896 | tf_op jit(solution)/shard_map/ppermute | solution.py:395
  749.1 360.6 %collective-permute-start.4 = (f32[96,2304]{1,0:T(8,128)}, f32[96,2304]{1,0:T(8,128)S(1)}, u32[]{:S(2)}, u32[]{:S(2)}) collective-permute-start(f32[96,2304]{1,0:T(8,128)} %reduce-scatter.9.cloned.1.call-done), channel_id=1, source_target_pairs={{4,0},{5,1},{6,2},{7,3}} | collective-permute-start | bytes 2654216 | tf_op jit(solution)/shard_map/ppermute | solution.py:400
  789.0 187.6 %collective-permute-start.6 = (f32[96,768]{1,0:T(8,128)}, f32[96,768]{1,0:T(8,128)S(1)}, u32[]{:S(2)}, u32[]{:S(2)}) collective-permute-start(f32[96,768]{1,0:T(8,128)} %reduce-scatter.13.cloned.1.call-done), channel_id=1, source_target_pairs={{4,0},{5,1},{6,2},{7,3}} | collective-permute-start | bytes 884744 | tf_op jit(solution)/shard_map/ppermute | solution.py:400
  826.7 215.3 %collective-permute-start.7 = (f32[96,768]{1,0:T(8,128)}, f32[96,768]{1,0:T(8,128)}, u32[]{:S(2)}, u32[]{:S(2)}) collective-permute-start(f32[96,768]{1,0:T(8,128)} %reduce-scatter.15.cloned.1.call-done), channel_id=1, source_target_pairs={{0,4},{1,5},{2,6},{3,7}} | collective-permute-start | bytes 884744 | tf_op jit(solution)/shard_map/ppermute | solution.py:400
  897.4 306.9 %collective-permute-start.10 = (f32[384,768]{1,0:T(8,128)}, f32[384,768]{1,0:T(8,128)}, u32[]{:S(2)}, u32[]{:S(2)}) collective-permute-start(f32[384,768]{1,0:T(8,128)} %reduce-scatter.21.cloned.1.call-done), channel_id=1, source_target_pairs={{4,0},{5,1},{6,2},{7,3}} | collective-permute-start | bytes 3538952 | tf_op jit(solution)/shard_map/ppermute | solution.py:400
  972.2 232.1 %collective-permute-start.11 = (f32[384,768]{1,0:T(8,128)}, f32[384,768]{1,0:T(8,128)}, u32[]{:S(2)}, u32[]{:S(2)}) collective-permute-start(f32[384,768]{1,0:T(8,128)} %reduce-scatter.23.cloned.1.call-done), channel_id=1, source_target_pairs={{0,4},{1,5},{2,6},{3,7}} | collective-permute-start | bytes 3538952 | tf_op jit(solution)/shard_map/ppermute | solution.py:400
  1037.6 160.0 %collective-permute-start.5 = (f32[96,2304]{1,0:T(8,128)}, f32[96,2304]{1,0:T(8,128)}, u32[]{:S(2)}, u32[]{:S(2)}) collective-permute-start(f32[96,2304]{1,0:T(8,128)} %reduce-scatter.11.cloned.1.call-done), channel_id=1, source_target_pairs={{0,4},{1,5},{2,6},{3,7}} | collective-permute-start | bytes 2654216 | tf_op jit(solution)/shard_map/ppermute | solution.py:400
  1108.4 99.4 %collective-permute-start.8 = (f32[96,3072]{1,0:T(8,128)}, f32[96,3072]{1,0:T(8,128)}, u32[]{:S(2)}, u32[]{:S(2)}) collective-permute-start(f32[96,3072]{1,0:T(8,128)} %reduce-scatter.17.cloned.1.call-done), channel_id=1, source_target_pairs={{4,0},{5,1},{6,2},{7,3}} | collective-permute-start | bytes 3538952 | tf_op jit(solution)/shard_map/ppermute | solution.py:400
  (18 other events, 282.5 us)
Sparse Core Ops, SparseCore 0:
  24.2 40.2 all-gather.8
  66.3 18.6 all-gather.10
  87.4 33.1 all-gather.12
  122.8 33.1 all-gather.14
  157.6 27.8 all-gather.16
  187.2 18.0 all-gather.18
  207.7 33.0 all-gather.20
  243.2 33.0 all-gather.22
  663.5 85.5 reduce-scatter.8
  752.8 36.1 reduce-scatter.12
  792.8 33.8 reduce-scatter.14
  830.0 67.4 reduce-scatter.20
  900.8 71.3 reduce-scatter.22
  975.5 62.0 reduce-scatter.10
  1040.9 67.4 reduce-scatter.16
  1111.6 71.4 reduce-scatter.18

commit v2 on v1

v2 whole, which is shorter than its diff:
```python
import functools
import math

import jax
import jax.numpy as jnp
from jax import lax
from jax.experimental import pallas as pl
from jax.experimental.pallas import tpu as pltpu
from jax.sharding import PartitionSpec as P


NORM_EPS = 1e-6
BF = jnp.bfloat16
F32 = jnp.float32
VMEM_LIMIT = 62 * 1024 * 1024
GELU_C = math.sqrt(2.0 / math.pi)
NN = (((1,), (0,)), ((), ()))
NT = (((1,), (1,)), ((), ()))
TN = (((0,), (0,)), ((), ()))


def dot(lhs, rhs, dims=NN):
    return lax.dot_general(lhs, rhs, dims, preferred_element_type=F32)


def rms_scale(hid_f32):
    return lax.rsqrt(jnp.mean(hid_f32 * hid_f32, axis=-1, keepdims=True) + NORM_EPS)


def rms_pull(hid_f32, scale, ct):
    inner = jnp.mean(ct * hid_f32, axis=-1, keepdims=True)
    return scale * (ct - hid_f32 * (scale * scale * inner))


def gelu_parts(pre):
    sq = pre * pre
    th = jnp.tanh(pre * (GELU_C + (GELU_C * 0.044715) * sq))
    half = 0.5 + 0.5 * th
    return sq, th, half


def head_masks(value):
    lane = lax.broadcasted_iota(jnp.int32, (1, 128), 1)
    low = jnp.where(lane < 64, value, 0.0).astype(BF)
    high = jnp.where(lane < 64, 0.0, value).astype(BF)
    return low, high


def causal_tile():
    return lax.broadcasted_iota(jnp.int32, (128, 128), 0) <= lax.broadcasted_iota(jnp.int32, (128, 128), 1)


def attn_fwd_kernel(off_ref, h_ref, w_ref, qkv_ref, attn_ref, lse_ref, held):
    step = pl.program_id(0)
    d_model = h_ref.shape[-1]
    hid = h_ref[...].astype(F32)
    normed = (hid * rms_scale(hid)).astype(BF)
    fresh = lax.rem(step, 2)
    ready = 1 - fresh

    def project(tile):
        cols = slice(tile * 256, (tile + 1) * 256)
        part = dot(normed, w_ref[:, cols]).astype(BF)
        qkv_ref[:, cols] = part
        held[fresh, :, cols] = part

    masks = head_masks(0.125)
    keep = causal_tile()
    zero_tile = jnp.zeros((128, 128), BF)
    heads = d_model // 64

    def score(head):
        base = (head // 2) * 128
        q_pair = held[ready, :, base:base + 128]
        k_pair = held[ready, :, d_model + base:d_model + base + 128]
        return dot(k_pair, q_pair * masks[head % 2], NT)

    tiles = 3 * d_model // 256
    scores = score(0)
    outs = []
    for head in range(heads):
        following = score(head + 1) if head + 1 < heads else None
        for tile in range(head * tiles // heads, (head + 1) * tiles // heads):
            project(tile)
        s00 = jnp.where(keep, scores[:128, :128], -1e30)
        s01 = scores[:128, 128:]
        s11 = jnp.where(keep, scores[128:, 128:], -1e30)
        top0 = jnp.max(s00, axis=0, keepdims=True)
        top1 = jnp.max(jnp.maximum(s01, s11), axis=0, keepdims=True)
        e00 = jnp.exp(s00 - top0)
        e01 = jnp.exp(s01 - top1)
        e11 = jnp.exp(s11 - top1)
        sum0 = jnp.sum(e00, axis=0, keepdims=True)
        sum1 = jnp.sum(e01 + e11, axis=0, keepdims=True)
        inv0 = 1.0 / sum0
        inv1 = 1.0 / sum1
        prob = jnp.concatenate([
            jnp.concatenate([(e00 * inv0).astype(BF), (e01 * inv1).astype(BF)], axis=1),
            jnp.concatenate([zero_tile, (e11 * inv1).astype(BF)], axis=1)], axis=0)
        lse_ref[head:head + 1, :] = jnp.concatenate([top0 + jnp.log(sum0), top1 + jnp.log(sum1)], axis=1)
        base = (head // 2) * 128
        if head % 2 == 0:
            v_tr = held[ready, :, 2 * d_model + base:2 * d_model + base + 128].T
        outs.append(dot(v_tr[(head % 2) * 64:(head % 2 + 1) * 64], prob))
        if head % 2 == 1:
            attn_ref[:, base:base + 128] = jnp.concatenate(outs, axis=0).T.astype(BF)
            outs = []
        scores = following


def attn_forward(offset, hidden, w_qkv, layer, seqs):
    _, seq_len, d_model = hidden.shape
    heads = d_model // 64
    flops = 2 * seqs * seq_len * d_model * 3 * d_model + 8 * seqs * heads * seq_len * seq_len * 128
    now = lambda i: jnp.minimum(i, seqs - 1)
    before = lambda i: jnp.maximum(i - 1, 0)
    return pl.pallas_call(
        attn_fwd_kernel,
        grid_spec=pltpu.PrefetchScalarGridSpec(
            num_scalar_prefetch=1,
            grid=(seqs + 1,),
            in_specs=[
                pl.BlockSpec((None, seq_len, d_model), lambda i, off: (now(i) + off[0] * seqs, 0, 0)),
                pl.BlockSpec((d_model, 3 * d_model), lambda i, off: (layer, 0), pipeline_mode=pl.Buffered(1)),
            ],
            out_specs=[
                pl.BlockSpec((None, seq_len, 3 * d_model), lambda i, off: (now(i), 0, 0)),
                pl.BlockSpec((None, seq_len, d_model), lambda i, off: (before(i), 0, 0)),
                pl.BlockSpec((None, heads, seq_len), lambda i, off: (before(i), 0, 0)),
            ],
            scratch_shapes=[pltpu.VMEM((2, seq_len, 3 * d_model), BF)],
        ),
        out_shape=[
            jax.ShapeDtypeStruct((seqs, seq_len, 3 * d_model), BF),
            jax.ShapeDtypeStruct((seqs, seq_len, d_model), BF),
            jax.ShapeDtypeStruct((seqs, heads, seq_len), F32),
        ],
        cost_estimate=pl.CostEstimate(flops=flops, bytes_accessed=40 << 20, transcendentals=0),
        compiler_params=pltpu.CompilerParams(vmem_limit_bytes=VMEM_LIMIT),
    )(offset, hidden, w_qkv)


def bundle_slices(d_model, d_ff, blocks):
    down, rows, parts = d_ff // blocks, d_model // blocks, d_ff // d_model
    pieces = []
    for blk in range(blocks):
        pieces.append(('proj', blk, pl.ds(down + parts * rows, rows), (pl.ds(blk * rows, rows), slice(None))))
    for part in range(parts):
        for blk in range(blocks):
            pieces.append((('up', part), blk, pl.ds(down + part * rows, rows), (pl.ds(blk * rows, rows), pl.ds(part * d_model, d_model))))
        for sub in range(blocks // parts):
            blk = part * (blocks // parts) + sub
            pieces.append((('down', part), blk, pl.ds(0, down), (pl.ds(blk * down, down), slice(None))))
    return pieces


def bundle_copies(bundle, proj, up, down, sems, to_bundle):
    found = {}
    for idx, (kind, blk, rows, spot) in enumerate(bundle_slices(proj.shape[0], up.shape[1], bundle.shape[0])):
        matrix = proj if kind == 'proj' else (up if kind[0] == 'up' else down)
        ends = (bundle.at[blk, rows, :], matrix.at[spot])
        src, dst = ends[::-1] if to_bundle else ends
        found.setdefault(kind, []).append(pltpu.make_async_copy(src, dst, sems.at[idx]))
    return found


def start_all(copies):
    for copy in copies:
        copy.start()


def wait_all(copies):
    for copy in copies:
        copy.wait()


def mlp_fwd_kernel(chunk, split, off_ref, h_ref, attn_ref, wb_ref, mid_ref, up_ref, *refs):
    out_refs, (wp_ref, wu_ref, wd_ref, sems) = refs[:-4], refs[-4:]
    first = pl.program_id(0) == 0
    loads = bundle_copies(wb_ref, wp_ref, wu_ref, wd_ref, sems, False)

    @pl.when(first)
    def _():
        for copies in loads.values():
            start_all(copies)
        wait_all(loads['proj'])

    mid = (h_ref[...].astype(F32) + dot(attn_ref[...], wp_ref[...])).astype(BF)
    mid_ref[...] = mid
    mid = mid.astype(F32)
    normed = (mid * rms_scale(mid)).astype(BF)
    total = mid

    @pl.when(first)
    def _():
        for kind, copies in loads.items():
            if kind != 'proj':
                wait_all(copies)

    for part in range(wu_ref.shape[1] // chunk):
        cols = slice(part * chunk, (part + 1) * chunk)
        up = dot(normed, wu_ref[:, cols]).astype(BF)
        up_ref[:, cols] = up
        pre = up.astype(F32)
        act = (pre * gelu_parts(pre)[2]).astype(BF)
        total = total + dot(act, wd_ref[cols, :])
    if split:
        own = off_ref[1] == 0
        half = split // 2
        for seq in range(total.shape[0] // split):
            lower = total[seq * split:seq * split + half]
            upper = total[seq * split + half:(seq + 1) * split]
            out_refs[0][seq] = jnp.where(own, lower, upper).astype(BF)
            out_refs[1][seq] = jnp.where(own, upper, lower).astype(BF)
    else:
        out_refs[0][...] = total.astype(BF)


def mlp_forward(offset, hidden, attn, bundle, d_ff, split=0, rows=512, chunk=768):
    tokens, d_model = attn.shape
    steps = tokens // rows
    flops = 2 * tokens * d_model * (d_model + 2 * d_ff)
    row_spec = pl.BlockSpec((rows, d_model), lambda i, off: (i, 0))
    pieces = len(bundle_slices(d_model, d_ff, bundle.shape[0]))
    return pl.pallas_call(
        functools.partial(mlp_fwd_kernel, chunk, split),
        grid_spec=pltpu.PrefetchScalarGridSpec(
            num_scalar_prefetch=1,
            grid=(steps,),
            in_specs=[pl.BlockSpec((rows, d_model), lambda i, off: (i + off[0] * steps, 0)), row_spec, pl.BlockSpec(memory_space=pl.ANY)],
            out_specs=[row_spec, pl.BlockSpec((rows, d_ff), lambda i, off: (i, 0))]
            + ([pl.BlockSpec((rows // split, split // 2, d_model), lambda i, off: (i, 0, 0))] * 2 if split else [row_spec]),
            scratch_shapes=[
                pltpu.VMEM((d_model, d_model), BF),
                pltpu.VMEM((d_model, d_ff), BF),
                pltpu.VMEM((d_ff, d_model), BF),
                pltpu.SemaphoreType.DMA((pieces,)),
            ],
        ),
        out_shape=[
            jax.ShapeDtypeStruct((tokens, d_model), BF),
            jax.ShapeDtypeStruct((tokens, d_ff), BF),
        ] + ([jax.ShapeDtypeStruct((tokens // split, split // 2, d_model), BF)] * 2 if split else [jax.ShapeDtypeStruct((tokens, d_model), BF)]),
        cost_estimate=pl.CostEstimate(flops=flops, bytes_accessed=50 << 20, transcendentals=0),
        compiler_params=pltpu.CompilerParams(vmem_limit_bytes=VMEM_LIMIT),
    )(offset, hidden, attn, bundle)


def mlp_bwd_kernel(chunk, off_ref, ct_ref, up_ref, mid_ref, wb_ref, ct_up_ref, g_out, wd_ref, gu_acc, gd_acc, in_sems, out_sems):
    step = pl.program_id(0)
    first = step == 0
    last = step == pl.num_programs(0) - 1
    d_model = ct_ref.shape[-1]
    blocks = wb_ref.shape[0]
    down = gd_acc.shape[0] // blocks
    rows = d_model // blocks
    ff_parts = gd_acc.shape[0] // d_model
    loads = [pltpu.make_async_copy(wb_ref.at[blk, pl.ds(0, down), :], wd_ref.at[pl.ds(blk * down, down), :], in_sems.at[blk]) for blk in range(blocks)]
    stores = []
    for blk in range(blocks):
        stores.append(pltpu.make_async_copy(gd_acc.at[pl.ds(blk * down, down), :], g_out.at[blk, pl.ds(0, down), :], out_sems.at[len(stores)]))
        for part in range(ff_parts):
            stores.append(pltpu.make_async_copy(gu_acc.at[pl.ds(blk * rows, rows), pl.ds(part * d_model, d_model)],
                                                g_out.at[blk, pl.ds(down + part * rows, rows), :], out_sems.at[len(stores)]))

    @pl.when(first)
    def _():
        start_all(loads)
        gd_acc[...] = jnp.zeros_like(gd_acc)
        gu_acc[...] = jnp.zeros_like(gu_acc)
        wait_all(loads)

    ct = ct_ref[...]
    mid = mid_ref[...].astype(F32)
    normed = (mid * rms_scale(mid)).astype(BF)

    def act_part(part):
        cols = slice(part * chunk, (part + 1) * chunk)
        ct_act = dot(ct, wd_ref[cols, :], NT).astype(BF).astype(F32)
        pre = up_ref[:, cols].astype(F32)
        sq, th, half = gelu_parts(pre)
        act = (pre * half).astype(BF)
        slope = half + (0.5 * pre) * (1.0 - th * th) * (GELU_C + (3.0 * 0.044715 * GELU_C) * sq)
        return act, (ct_act * slope).astype(BF)

    parts = wd_ref.shape[0] // chunk
    now = act_part(0)
    for part in range(parts):
        cols = slice(part * chunk, (part + 1) * chunk)
        act, ct_up = now
        ct_up_ref[:, cols] = ct_up
        now = act_part(part + 1) if part + 1 < parts else None
        gd_acc[cols, :] += dot(act, ct, TN)
        gu_acc[:, cols] += dot(normed, ct_up, TN)

    @pl.when(last)
    def _():
        start_all(stores)
        wait_all(stores)


def mlp_backward(offset, ct, up, mid, bundle, rows=512, chunk=768):
    tokens, d_model = mid.shape
    d_ff = up.shape[1]
    steps = tokens // rows
    blocks = bundle.shape[0]
    row_spec = pl.BlockSpec((rows, d_model), lambda i, off: (i, 0))
    wide_spec = pl.BlockSpec((rows, d_ff), lambda i, off: (i, 0))
    hbm = pl.BlockSpec(memory_space=pl.ANY)
    return pl.pallas_call(
        functools.partial(mlp_bwd_kernel, chunk),
        grid_spec=pltpu.PrefetchScalarGridSpec(
            num_scalar_prefetch=1,
            grid=(steps,),
            in_specs=[pl.BlockSpec((rows, d_model), lambda i, off: (i + off[0] * steps, 0)), wide_spec, row_spec, hbm],
            out_specs=[wide_spec, hbm],
            scratch_shapes=[
                pltpu.VMEM((d_ff, d_model), BF),
                pltpu.VMEM((d_model, d_ff), F32),
                pltpu.VMEM((d_ff, d_model), F32),
                pltpu.SemaphoreType.DMA((blocks,)),
                pltpu.SemaphoreType.DMA((blocks * (1 + d_ff // d_model),)),
            ],
        ),
        out_shape=[
            jax.ShapeDtypeStruct((tokens, d_ff), BF),
            jax.ShapeDtypeStruct((blocks, 2 * d_ff // blocks, d_model), F32),
        ],
        cost_estimate=pl.CostEstimate(flops=6 * tokens * d_model * d_ff, bytes_accessed=70 << 20, transcendentals=0),
        compiler_params=pltpu.CompilerParams(vmem_limit_bytes=VMEM_LIMIT),
    )(offset, ct, up, mid, bundle)


def attn_bwd_kernel(with_input, *refs):
    if with_input:
        off_ref, h_ref, qkv_ref, lse_ref, ct_up_ref, mid_ref, ct_ref, attn_ref, wb_ref, w_ref, ct_h_ref, g_out, ct_attn, dqkv, wp_ref, wu_ref, g_acc, sems = refs
    else:
        off_ref, h_ref, qkv_ref, lse_ref, ct_up_ref, mid_ref, ct_ref, attn_ref, wb_ref, g_out, ct_attn, dqkv, wp_ref, wu_ref, g_acc, sems = refs
    step = pl.program_id(0)
    last = step == pl.num_programs(0) - 1
    d_model = h_ref.shape[-1]
    blocks = wb_ref.shape[0]
    rows = d_model // blocks
    ff_parts = wu_ref.shape[1] // d_model
    down = wb_ref.shape[1] - rows * (1 + ff_parts)
    loads = []
    for blk in range(blocks):
        spot = pl.ds(blk * rows, rows)
        for part in range(ff_parts):
            loads.append(pltpu.make_async_copy(wb_ref.at[blk, pl.ds(down + part * rows, rows), :], wu_ref.at[spot, pl.ds(part * d_model, d_model)], sems.at[len(loads)]))
        loads.append(pltpu.make_async_copy(wb_ref.at[blk, pl.ds(down + ff_parts * rows, rows), :], wp_ref.at[spot, :], sems.at[len(loads)]))

    @pl.when(step == 0)
    def _():
        start_all(loads)
        g_acc[...] = jnp.zeros_like(g_acc)
        wait_all(loads)

    mid = mid_ref[...].astype(F32)
    ct_norm2 = dot(ct_up_ref[...], wu_ref[...], NT).astype(BF).astype(F32)
    ct_mid = (ct_ref[...].astype(F32) + rms_pull(mid, rms_scale(mid), ct_norm2)).astype(BF)
    ct_attn[...] = dot(ct_mid, wp_ref[...], NT).astype(BF)
    g_acc[:, 3 * d_model:] += dot(attn_ref[...], ct_mid, TN)

    q_masks = head_masks(0.125)
    o_masks = head_masks(1.0)
    keep = causal_tile()
    zero_tile = jnp.zeros((128, 128), BF)

    def square(t00, t01, t11):
        return jnp.concatenate([
            jnp.concatenate([t00.astype(BF), t01.astype(BF)], axis=1),
            jnp.concatenate([zero_tile, t11.astype(BF)], axis=1)], axis=0)

    def begin(head):
        base = (head // 2) * 128
        k_pair = qkv_ref[:, d_model + base:d_model + base + 128]
        v_pair = qkv_ref[:, 2 * d_model + base:2 * d_model + base + 128]
        q_sub = qkv_ref[:, base:base + 128] * q_masks[head % 2]
        o_sub = ct_attn[:, base:base + 128] * o_masks[head % 2]
        return q_sub, o_sub, dot(k_pair, q_sub, NT), dot(v_pair, o_sub, NT)

    heads = d_model // 64
    now = begin(0)
    for head in range(heads):
        following = begin(head + 1) if head + 1 < heads else None
        base = (head // 2) * 128
        q_sub, o_sub, scores, d_prob = now
        if head % 2 == 0:
            k_tr = qkv_ref[:, d_model + base:d_model + base + 128].T
            dq_parts = []
        lse0 = lse_ref[head:head + 1, :128]
        lse1 = lse_ref[head:head + 1, 128:]
        p00 = jnp.exp(jnp.where(keep, scores[:128, :128] - lse0, -1e30))
        p01 = jnp.exp(scores[:128, 128:] - lse1)
        p11 = jnp.exp(jnp.where(keep, scores[128:, 128:] - lse1, -1e30))
        d00 = d_prob[:128, :128].astype(BF).astype(F32)
        d01 = d_prob[:128, 128:].astype(BF).astype(F32)
        d11 = d_prob[128:, 128:].astype(BF).astype(F32)
        m0 = jnp.sum(p00 * d00, axis=0, keepdims=True)
        m1 = jnp.sum(p01 * d01 + p11 * d11, axis=0, keepdims=True)
        d_score = square(p00 * (d00 - m0), p01 * (d01 - m1), p11 * (d11 - m1))
        dv_sub = dot(square(p00, p01, p11), o_sub)
        dk_sub = dot(d_score, q_sub)
        dq_parts.append(dot(k_tr[(head % 2) * 64:(head % 2 + 1) * 64], d_score))
        if head % 2 == 0:
            dv_pair, dk_pair = dv_sub, dk_sub
        else:
            dqkv[:, base:base + 128] = (jnp.concatenate(dq_parts, axis=0).T * 0.125).astype(BF)
            dqkv[:, d_model + base:d_model + base + 128] = (dk_pair + dk_sub).astype(BF)
            dqkv[:, 2 * d_model + base:2 * d_model + base + 128] = (dv_pair + dv_sub).astype(BF)
        now = following

    hid = h_ref[...].astype(F32)
    scale = rms_scale(hid)
    normed = (hid * scale).astype(BF)
    for part in range(3):
        cols = slice(part * d_model, (part + 1) * d_model)
        g_acc[:, cols] += dot(normed, dqkv[:, cols], TN)
    if with_input:
        ct_norm = dot(dqkv[...], w_ref[...], NT).astype(BF).astype(F32)
        ct_h_ref[...] = (ct_mid.astype(F32) + rms_pull(hid, scale, ct_norm)).astype(BF)

    @pl.when(last)
    def _():
        copy = pltpu.make_async_copy(g_acc, g_out, sems.at[len(loads)])
        copy.start()
        copy.wait()


def attn_backward(offsets, hidden, qkv, lse, ct_up, mid, ct, attn, bundle, w_qkv, with_input):
    seqs, seq_len = qkv.shape[:2]
    d_model, d_ff = hidden.shape[-1], ct_up.shape[-1]
    heads = d_model // 64
    blocks = bundle.shape[0]
    flops = 2 * seqs * seq_len * d_model * (d_ff + d_model * (8 if with_input else 5)) + 20 * seqs * heads * seq_len * seq_len * 128
    block = lambda width, which=None: pl.BlockSpec((None, seq_len, width), (lambda i, off: (i, 0, 0)) if which is None else (lambda i, off: (i + off[which] * seqs, 0, 0)))
    hbm = pl.BlockSpec(memory_space=pl.ANY)
    in_specs = [block(d_model, 0), block(3 * d_model), pl.BlockSpec((None, heads, seq_len), lambda i, off: (i, 0, 0)),
                block(d_ff), block(d_model), block(d_model, 1), block(d_model), hbm]
    args = [offsets, hidden, qkv, lse, ct_up, mid, ct, attn, bundle]
    out_specs = [hbm]
    out_shape = [jax.ShapeDtypeStruct((d_model, 4 * d_model), F32)]
    if with_input:
        in_specs.append(pl.BlockSpec((d_model, 3 * d_model), lambda i, off: (1, 0), pipeline_mode=pl.Buffered(1)))
        args.append(w_qkv)
        out_specs = [block(d_model)] + out_specs
        out_shape = [jax.ShapeDtypeStruct((seqs, seq_len, d_model), BF)] + out_shape
    return pl.pallas_call(
        functools.partial(attn_bwd_kernel, with_input),
        grid_spec=pltpu.PrefetchScalarGridSpec(
            num_scalar_prefetch=1,
            grid=(seqs,),
            in_specs=in_specs,
            out_specs=out_specs,
            scratch_shapes=[
                pltpu.VMEM((seq_len, d_model), BF),
                pltpu.VMEM((seq_len, 3 * d_model), BF),
                pltpu.VMEM((d_model, d_model), BF),
                pltpu.VMEM((d_model, d_ff), BF),
                pltpu.VMEM((d_model, 4 * d_model), F32),
                pltpu.SemaphoreType.DMA((blocks * (1 + d_ff // d_model) + 1,)),
            ],
        ),
        out_shape=out_shape,
        cost_estimate=pl.CostEstimate(flops=flops, bytes_accessed=50 << 20, transcendentals=0),
        compiler_params=pltpu.CompilerParams(vmem_limit_bytes=VMEM_LIMIT),
    )(*args)


def solution(mesh):
    stages = mesh.shape['pp']
    both = ('dp', 'pp')
    swap = [(0, 1), (1, 0)]

    def device_step(act_in, loss_seed, w_qkv, w_proj, w_up, w_down):
        stage = lax.axis_index('pp')
        micro = act_in.shape[0] // stages
        seq_len, d_model = act_in.shape[2:]
        d_ff = w_up.shape[2]
        ff_parts = d_ff // d_model
        seqs = micro * act_in.shape[1]
        tokens = seqs * seq_len
        own = stage.astype(jnp.int32).reshape(1)
        zero = jnp.zeros((1,), jnp.int32)

        wq_shard = w_qkv.reshape(-1, 3 * d_model)
        wq = lax.all_gather(wq_shard, ('pp', 'dp'), axis=0, tiled=True)
        w_proj, w_up, w_down, _ = lax.optimization_barrier((w_proj, w_up, w_down, wq_shard))

        rows = w_proj.shape[1] // 2
        mlp_halves = jnp.concatenate(
            [w_down[0].reshape(2, -1, d_model)]
            + [w_up[0, :, part * d_model:(part + 1) * d_model].reshape(2, rows, d_model) for part in range(ff_parts)]
            + [w_proj[0].reshape(2, rows, d_model)], axis=1)
        kept = lax.dynamic_index_in_dim(mlp_halves, stage, 0, keepdims=False)
        got = lax.ppermute(lax.dynamic_index_in_dim(mlp_halves, 1 - stage, 0, keepdims=False), 'pp', swap)
        bundles = []
        for layer in range(2):
            bundles.append(lax.all_gather(jnp.where(stage == layer, kept, got), both, axis=0))

        hidden = act_in.reshape(stages * seqs, seq_len, d_model)
        saved = []
        for layer in range(2):
            off = own if layer == 0 else zero
            wb = bundles[layer]
            qkv, attn, lse = attn_forward(off, hidden, wq, layer, seqs)
            attn = attn.reshape(tokens, d_model)
            offs = jnp.concatenate([off, own])
            mid, up, *outs = mlp_forward(offs, hidden.reshape(-1, d_model), attn, wb, d_ff, split=seq_len if layer == 1 else 0)
            saved.append((hidden, qkv, attn, lse, mid, up))
            hidden = outs[0].reshape(seqs, -1, d_model)
        half_shape = (micro, act_in.shape[1], seq_len // 2, d_model)
        final_kept, final_sent = [out.reshape(half_shape) for out in outs]
        final_got = lax.ppermute(final_sent, 'pp', swap)
        act_out = jnp.where(stage == 0, jnp.concatenate([final_kept, final_got]), jnp.concatenate([final_got, final_kept]))

        def reduce_rows(grad, layer):
            block = lax.psum_scatter(grad, both, scatter_dimension=0, tiled=True)
            got = lax.ppermute(block, 'pp', [(1 - layer, layer)])
            return (block, got) if layer == 0 else (got, block)

        def reduce_stage(grad, layer):
            block = lax.psum_scatter(grad, 'dp', scatter_dimension=0, tiled=True)
            got = lax.ppermute(block, 'pp', [(1 - layer, layer)])
            return block, got

        ct = loss_seed.reshape(stages * tokens, d_model)
        shape3 = (-1, seq_len, d_model)
        reduced = [None, None]
        for layer in (1, 0):
            wb = bundles[layer]
            hid, qkv, attn, lse, mid, up = saved[layer]
            ct_up, g_mlp = mlp_backward(own if layer == 1 else zero, ct, up, mid, wb)
            if layer == 0:
                ct_up, act_out = lax.optimization_barrier((ct_up, act_out))
            mlp_part = reduce_rows(g_mlp, layer)
            offsets = jnp.concatenate([zero, own] if layer == 1 else [own, zero])
            res = attn_backward(offsets, hid, qkv, lse, ct_up.reshape(seqs, seq_len, d_ff), mid.reshape(shape3), ct.reshape(shape3), attn.reshape(shape3),
                                wb, wq, layer > 0)
            attn_part = reduce_stage(res[-1], layer)
            reduced[layer] = (mlp_part, attn_part)
            if layer == 1:
                ct = res[0].reshape(tokens, d_model)
        pick = lambda first, second: jnp.where(stage == 0, first, second)
        mlp = [pick(reduced[0][0][half], reduced[1][0][half]).reshape(-1, d_model) for half in range(2)]
        wide = pick(*[sum(reduced[layer][1]) for layer in range(2)])
        down = d_ff // (2 * mesh.shape['dp'])
        gd = jnp.concatenate([half[:down] for half in mlp])
        gu = jnp.concatenate([jnp.concatenate([half[down + part * rows:down + (part + 1) * rows] for part in range(ff_parts)], axis=1) for half in mlp])
        gq, gp = wide[:, :3 * d_model], wide[:, 3 * d_model:]
        return gq.reshape(w_qkv.shape), gp[None], gu[None], gd[None], act_out

    weight_spec = P('pp', 'dp')
    act_spec = P(None, 'dp')
    return jax.shard_map(device_step, mesh=mesh, in_specs=(act_spec, act_spec, weight_spec, weight_spec, weight_spec, weight_spec), out_specs=(weight_spec, weight_spec, weight_spec, weight_spec, P(None, 'dp', 'pp')), check_vma=False)
```

time: 1220 us -> 1040 us (0.85); the launches traced: 1220 us -> 1030 us
  waiting for transfers between devices: 580 us -> 453 us
  Pallas kernels: 549 us -> 512 us
  starting transfers between devices: 33.8 us -> 14.9 us
    reduce_scatter x8 -> x2, waiting for transfers between devices: 492 us -> 274 us  [reduce_rows(): block = lax.psum_scatter(grad, both, scatter_dimension=0, tiled=True)]
    reduce_scatter x0 -> x2, waiting for transfers between devices: none -> 68.4 us  [reduce_stage(): block = lax.psum_scatter(grad, 'dp', scatter_dimension=0, tiled=True)]
    pallas_call x8, Pallas kernels: 549 us -> 512 us  [the longest x2 191 us: attn_backward(): pl.pallas_call(functools.partial(attn_bwd_kernel, with_input), grid_spec=...]
    ppermute x8 -> x2, waiting for transfers between devices: 3.68 us -> 35.9 us  [reduce_rows(): got = lax.ppermute(block, 'pp', [(1 - layer, layer)])]
    ppermute x8 -> x2, starting transfers between devices: 22.4 us -> 6.05 us  [reduce_rows(): got = lax.ppermute(block, 'pp', [(1 - layer, layer)])]
    dynamic_slice x7 -> x0, local copies, waits for them, and re-layouts: 16 us -> none  [the longest x1 4.83 us: device_step(): lax.dynamic_slice_in_dim(act_in, stage * micro, micro, 0)]
    all_gather x8 -> x3, waiting for transfers between devices: 30.5 us -> 21.5 us  [the longest x2 18.3 us: device_step(): lax.all_gather(jnp.where(stage == layer, kept, got), both, axis=0)]
    ppermute x5 -> x4, waiting for transfers between devices: 47.9 us -> 51.4 us  [the longest x1 51.4 us: device_step(): lax.ppermute(lax.dynamic_index_in_dim(mlp_halves, 1 - stage, 0, keepdims=...]
  transfers between devices with their start and end apart: 29 -> 13, of which waited for: 15 -> 7; matrix products, arithmetic and copies ran while one was open for 3% -> 3% of each run, Pallas kernels for 13% -> 28%
where the time goes in v2:
time: 1040 us; the launch traced here: 1030 us
  Pallas kernels  512 us (49%)
  waiting for transfers between devices  453 us (44%)
  other arithmetic  21.8 us (2%)
  starting transfers between devices  14.9 us (1%)
  between operations  14.5 us (1%)
  local copies, waits for them, and re-layouts  13.1 us (1%)
    reduce_scatter x2, waiting for transfers between devices, reduce_rows(): block = lax.psum_scatter(grad, both, scatter_dimension=0, tiled=True)  274 us
    pallas_call x2, Pallas kernels, attn_backward(): pl.pallas_call(functools.partial(attn_bwd_kernel, with_input), grid_spec=...  191 us
    pallas_call x2, Pallas kernels, mlp_backward(): pl.pallas_call(functools.partial(mlp_bwd_kernel, chunk), grid_spec=pltpu....  142 us
    pallas_call x2, Pallas kernels, mlp_forward(): pl.pallas_call(functools.partial(mlp_fwd_kernel, chunk, split), grid_spec...  92.1 us
    pallas_call x2, Pallas kernels, attn_forward(): pl.pallas_call(attn_fwd_kernel, grid_spec=pltpu.PrefetchScalarGridSpec(nu...  87 us
    reduce_scatter x2, waiting for transfers between devices, reduce_stage(): block = lax.psum_scatter(grad, 'dp', scatter_dimension=0, tiled=True)  68.4 us
    ppermute x1, waiting for transfers between devices, device_step(): lax.ppermute(lax.dynamic_index_in_dim(mlp_halves, 1 - stage, 0, keepdims=...  51.4 us
    ppermute x2, waiting for transfers between devices, reduce_rows(): got = lax.ppermute(block, 'pp', [(1 - layer, layer)])  35.9 us
  transfers between devices with their start and end apart: 13, of which 7 were waited for; matrix products, arithmetic and copies ran while one was open for 3% of the time, Pallas kernels for 28%

profile of v2, /device:TPU:0, one launch (start us, length us, event | category | flops | bytes accessed | tf_op | source)
XLA Modules:
  0.0 1029.4 jit_solution(3058364325485385319)
XLA Ops:
  7.2 2.3 copy.13
  13.6 3.3 collective-permute-start
  17.0 51.4 %collective-permute-done = bf16[864,768]{1,0:T(8,128)(2,1)} collective-permute-done((bf16[864,768]{1,0:T(8,128)(2,1)}, bf16[864,768]{1,0:T(8,128)(2,1)}, u32[]{:S(2)}, u32[]{:S(2)}) %collective-permute-start) | collective-permute-done | bytes 1327136 | tf_op jit(solution)/shard_map/ppermute | solution.py:497
  68.4 3.0 bitcast_select_fusion
  73.4 3.2 all-gather.6.cloned.1.call-done.w_ref.refs_9_
  76.6 43.5 %shard_map.101 = (bf16[12,256,2304]{2,1,0:T(8,128)(2,1)}, bf16[12,256,768]{2,1,0:T(8,128)(2,1)}, f32[12,12,256]{2,1,0:T(8,128)}) custom-call(s32[1]{0:T(128)} %bitcast.off_ref, bf16[24,256,768]{2,1,0:T(8,128)(2,1)} %bitcast.73, bf16[1536,2304]{1,0:T(8,128)(2,1)} %all-gather.6.cloned.1.call-done.w_ref.refs_9_), custom_call_target="tpu_custom_call" | custom-call | flops 20535312384 | bytes 41943040 | tf_op jit(solution)/shard_map/pallas_call | solution.py:117
  120.1 18.3 %all-gather.8.cloned.1.call-done = bf16[6912,768]{1,0:T(8,128)(2,1)} async-done(((bf16[864,768]{1,0:T(8,128)(2,1)}), bf16[6912,768]{1,0:T(8,128)(2,1)}) %all-gather.8.cloned.1.call-update) | async-done | bytes 10616848 | tf_op jit(solution)/shard_map/all_gather | solution.py:500
  138.4 45.9 %shard_map.102 = (bf16[3072,768]{1,0:T(8,128)(2,1)}, bf16[3072,3072]{1,0:T(8,128)(2,1)}, bf16[3072,768]{1,0:T(8,128)(2,1)}) custom-call(s32[2]{0:T(128)} %pad_add_fusion.2.off_ref, bf16[6144,768]{1,0:T(8,128)(2,1)} %bitcast.74, bf16[3072,768]{1,0:T(8,128)(2,1)} %bitcast.78, bf16[8,864,768]{2,1,0:T(8,128)(2,1)} %bitcast.65), custom_call_target="tpu_custom_call" | custom-call | flops 32614907904 | bytes 52428800 | tf_op jit(solution)/shard_map/pallas_call | solution.py:225
  184.2 43.5 %shard_map.103 = (bf16[12,256,2304]{2,1,0:T(8,128)(2,1)}, bf16[12,256,768]{2,1,0:T(8,128)(2,1)}, f32[12,12,256]{2,1,0:T(8,128)}) custom-call(s32[1]{0:T(128)} %constant.17.clone.1.off_ref, bf16[12,256,768]{2,1,0:T(8,128)(2,1)} %bitcast.81, bf16[1536,2304]{1,0:T(8,128)(2,1)} %all-gather.6.cloned.1.call-done.w_ref.refs_9_), custom_call_target="tpu_custom_call" | custom-call | flops 20535312384 | bytes 41943040 | tf_op jit(solution)/shard_map/pallas_call | solution.py:117
  227.7 46.2 %shard_map.104 = (bf16[3072,768]{1,0:T(8,128)(2,1)}, bf16[3072,3072]{1,0:T(8,128)(2,1)}, bf16[12,128,768]{2,1,0:T(8,128)(2,1)}, bf16[12,128,768]{2,1,0:T(8,128)(2,1)}) custom-call(s32[2]{0:T(128)} %pad_add_fusion.1.off_ref.refs_0_, bf16[3072,768]{1,0:T(8,128)(2,1)} %get-tuple-element.35.h_ref, bf16[3072,768]{1,0:T(8,128)(2,1)} %bitcast.83, ...), custom_call_target="tpu_custom_call" | custom-call | flops 32614907904 | bytes 52428800 | tf_op jit(solution)/shard_map/pallas_call | solution.py:225
  274.0 69.7 %shard_map.105 = (bf16[3072,3072]{1,0:T(8,128)(2,1)}, f32[8,768,768]{2,1,0:T(8,128)}) custom-call(s32[1]{0:T(128)} %bitcast.off_ref, bf16[6144,768]{1,0:T(8,128)(2,1)} %bitcast.71, bf16[3072,3072]{1,0:T(8,128)(2,1)} %get-tuple-element.39.up_ref, bf16[3072,768]{1,0:T(8,128)(2,1)} %get-tuple-element.40.mid_ref, bf16[8,864,768]{2,1,0:T(8,128)(2,1)} %bitcast.69), custom_call_target="tpu_custom_call" | custom-call | flops 43486543872 | bytes 73400320 | tf_op jit(solution)/shard_map/pallas_call | solution.py:310
  343.7 105.0 %shard_map.106 = (bf16[12,256,768]{2,1,0:T(8,128)(2,1)}, f32[768,3072]{1,0:T(8,128)}) custom-call(s32[2]{0:T(128)} %pad_add_fusion.1.off_ref.refs_0_, bf16[12,256,768]{2,1,0:T(8,128)(2,1)} %bitcast.82, bf16[12,256,2304]{2,1,0:T(8,128)(2,1)} %get-tuple-element.36.refs_2_, f32[12,12,256]{2,1,0:T(8,128)} %get-tuple-element.37.refs_3_, ...), custom_call_target="tpu_custom_call" | custom-call | flops 67645734912 | bytes 52428800 | tf_op jit(solution)/shard_map/pallas_call | solution.py:449
  450.3 72.8 %shard_map.107 = (bf16[3072,3072]{1,0:T(8,128)(2,1)}, f32[8,768,768]{2,1,0:T(8,128)}) custom-call(s32[1]{0:T(128)} %constant.17.clone.1.off_ref, bf16[3072,768]{1,0:T(8,128)(2,1)} %bitcast.80, bf16[3072,3072]{1,0:T(8,128)(2,1)} %get-tuple-element.43.up_ref, bf16[3072,768]{1,0:T(8,128)(2,1)} %get-tuple-element.44.mid_ref, bf16[8,864,768]{2,1,0:T(8,128)(2,1)} %bitcast.66), custom_call_target="tpu_custom_call" | custom-call | flops 43486543872 | bytes 73400320 | tf_op jit(solution)/shard_map/pallas_call | solution.py:310
  523.1 6.9 maximum_select_fusion
  530.0 85.7 %shard_map.108 = f32[768,3072]{1,0:T(8,128)} custom-call(s32[2]{0:T(128)} %pad_add_fusion.refs_0_, bf16[24,256,768]{2,1,0:T(8,128)(2,1)} %bitcast.75, bf16[12,256,2304]{2,1,0:T(8,128)(2,1)} %get-tuple-element.29.refs_2_, f32[12,12,256]{2,1,0:T(8,128)} %get-tuple-element.30.refs_3_, bf16[12,256,3072]{2,1,0:T(8,128)(2,1)} %bitcast.76, ...), custom_call_target="tpu_custom_call" | custom-call | flops 56774098944 | bytes 52428800 | tf_op jit(solution)/shard_map/pallas_call | solution.py:449
  617.0 3.0 collective-permute-start.3
  620.0 68.4 %reduce-scatter.5.cloned.1.call-done = f32[192,3072]{1,0:T(8,128)} async-done(((f32[768,3072]{1,0:T(8,128)}), f32[192,3072]{1,0:T(8,128)}) %reduce-scatter.5.cloned.1.call-update) | async-done | bytes 2359312 | tf_op jit(solution)/shard_map/reduce_scatter | solution.py:524
  689.7 136.4 %reduce-scatter.9.cloned.1.call-done = f32[1,768,768]{2,1,0:T(8,128)} async-done(((f32[8,768,768]{2,1,0:T(8,128)}), f32[1,768,768]{2,1,0:T(8,128)}) %reduce-scatter.9.cloned.1.call-update) | async-done | bytes 2359312 | tf_op jit(solution)/shard_map/reduce_scatter | solution.py:519
  827.4 137.2 %reduce-scatter.11.cloned.1.call-done = f32[1,768,768]{2,1,0:T(8,128)} async-done(((f32[8,768,768]{2,1,0:T(8,128)}), f32[1,768,768]{2,1,0:T(8,128)}) %reduce-scatter.11.cloned.1.call-update) | async-done | bytes 2359312 | tf_op jit(solution)/shard_map/reduce_scatter | solution.py:519
  964.6 4.8 collective-permute-start.4
  970.8 4.6 add_select_fusion
  976.7 2.9 copy.14
  980.5 2.0 broadcast_select_fusion
  982.7 35.9 %collective-permute-done.4 = f32[1,768,768]{2,1,0:T(8,128)} collective-permute-done((f32[1,768,768]{2,1,0:T(8,128)}, f32[1,768,768]{2,1,0:T(8,128)}, u32[]{:S(2)}, u32[]{:S(2)}) %collective-permute-start.4) | collective-permute-done | bytes 2359328 | tf_op jit(solution)/shard_map/ppermute | solution.py:520
  (49 shorter events, 19.1 us)
Async XLA Ops:
  7.2 69.5 %all-gather.6.cloned.1.call-start = ((), (), s32[]{:S(2)}) async-start(), calls=%async_computation.4 | async-start | bytes 7962624 | tf_op jit(solution)/shard_map/all_gather | solution.py:488
  9.5 128.8 %all-gather.8.cloned.1.call-start = ((), (), s32[]{:S(2)}) async-start(), calls=%async_computation.9 | async-start | bytes 11943936 | tf_op jit(solution)/shard_map/all_gather | solution.py:500
  10.9 1.5 copy-start.2
  13.6 54.7 %collective-permute-start = (bf16[864,768]{1,0:T(8,128)(2,1)}, bf16[864,768]{1,0:T(8,128)(2,1)}, u32[]{:S(2)}, u32[]{:S(2)}) collective-permute-start(bf16[864,768]{1,0:T(8,128)(2,1)} %dynamic-slice_bitcast_fusion), channel_id=1, source_target_pairs={{0,4},{4,0},{1,5},{5,1},{2,6},{6,2},{3,7},{7,3}} | collective-permute-start | bytes 3981320 | tf_op jit(solution)/shard_map/ppermute | solution.py:497
  71.4 156.4 %all-gather.10.cloned.1.call-start = ((), (), s32[]{:S(2)}) async-start(), calls=%async_computation.10 | async-start | bytes 11943936 | tf_op jit(solution)/shard_map/all_gather | solution.py:500
  72.1 544.9 %reduce-scatter.7.cloned.1.call-start = ((), (), s32[]{:S(2)}) async-start(), calls=%async_computation.6 | async-start | bytes 11796480 | tf_op jit(solution)/shard_map/reduce_scatter | solution.py:524
  448.7 239.7 %reduce-scatter.5.cloned.1.call-start = ((), (), s32[]{:S(2)}) async-start(), calls=%async_computation.5 | async-start | bytes 11796480 | tf_op jit(solution)/shard_map/reduce_scatter | solution.py:524
  449.4 73.7 %collective-permute-start.1 = (bf16[2,6,128,768]{3,2,1,0:T(8,128)(2,1)}, bf16[2,6,128,768]{3,2,1,0:T(8,128)(2,1)}, u32[]{:S(2)}, u32[]{:S(2)}) collective-permute-start(bf16[2,6,128,768]{3,2,1,0:T(8,128)(2,1)} %bitcast.23), channel_id=1, source_target_pairs={{0,4},{4,0},{1,5},{5,1},{2,6},{6,2},{3,7},{7,3}} | collective-permute-start | bytes 7077896 | tf_op jit(solution)/shard_map/ppermute | solution.py:515
  615.7 210.4 %reduce-scatter.9.cloned.1.call-start = ((), (), s32[]{:S(2)}) async-start(), calls=%async_computation.7 | async-start | bytes 21233664 | tf_op jit(solution)/shard_map/reduce_scatter | solution.py:519
  616.3 348.4 %reduce-scatter.11.cloned.1.call-start = ((), (), s32[]{:S(2)}) async-start(), calls=%async_computation.8 | async-start | bytes 21233664 | tf_op jit(solution)/shard_map/reduce_scatter | solution.py:519
  617.0 352.4 %collective-permute-start.3 = (f32[192,3072]{1,0:T(8,128)}, f32[192,3072]{1,0:T(8,128)S(1)}, u32[]{:S(2)}, u32[]{:S(2)}) collective-permute-start(f32[192,3072]{1,0:T(8,128)} %reduce-scatter.7.cloned.1.call-done), channel_id=1, source_target_pairs={{0,4},{1,5},{2,6},{3,7}} | collective-permute-start | bytes 7077896 | tf_op jit(solution)/shard_map/ppermute | solution.py:525
  688.4 282.4 %collective-permute-start.2 = (f32[192,3072]{1,0:T(8,128)}, f32[192,3072]{1,0:T(8,128)}, u32[]{:S(2)}, u32[]{:S(2)}) collective-permute-start(f32[192,3072]{1,0:T(8,128)} %reduce-scatter.5.cloned.1.call-done), channel_id=1, source_target_pairs={{4,0},{5,1},{6,2},{7,3}} | collective-permute-start | bytes 7077896 | tf_op jit(solution)/shard_map/ppermute | solution.py:525
  826.1 154.4 %collective-permute-start.5 = (f32[1,768,768]{2,1,0:T(8,128)}, f32[1,768,768]{2,1,0:T(8,128)}, u32[]{:S(2)}, u32[]{:S(2)}) collective-permute-start(f32[1,768,768]{2,1,0:T(8,128)} %reduce-scatter.9.cloned.1.call-done), channel_id=1, source_target_pairs={{4,0},{5,1},{6,2},{7,3}} | collective-permute-start | bytes 7077896 | tf_op jit(solution)/shard_map/ppermute | solution.py:520
  964.6 54.0 %collective-permute-start.4 = (f32[1,768,768]{2,1,0:T(8,128)}, f32[1,768,768]{2,1,0:T(8,128)}, u32[]{:S(2)}, u32[]{:S(2)}) collective-permute-start(f32[1,768,768]{2,1,0:T(8,128)} %reduce-scatter.11.cloned.1.call-done), channel_id=1, source_target_pairs={{0,4},{1,5},{2,6},{3,7}} | collective-permute-start | bytes 7077896 | tf_op jit(solution)/shard_map/ppermute | solution.py:520
  969.4 1.4 copy-start.1
  982.5 36.1 %copy-start = (f32[1,768,768]{2,1,0:T(8,128)S(1)}, f32[1,768,768]{2,1,0:T(8,128)}, u32[]{:S(2)}) copy-start(f32[1,768,768]{2,1,0:T(8,128)} %reduce-scatter.9.cloned.1.call-done) | copy-start | bytes 7077892
Sparse Core Ops, SparseCore 0:
  10.4 66.2 all-gather.5
  79.0 59.3 all-gather.7
  140.8 58.1 all-gather.9
  448.9 72.2 reduce-scatter.6
  615.8 72.5 reduce-scatter.4
  691.8 134.2 reduce-scatter.8
  829.7 134.9 reduce-scatter.10
